TPU v7x, 32 devices: a whole 2x2x4 slice. The times are simulated.
32 devices in a mesh: col: 8 (over z, y), row: 4 (over x, core).
Axes of the slice: x: 2, y: 2, z: 4, core: 2. Of those that a mesh axis runs over, the one named last changes fastest.
Arguments:
- right_side: float32 [8192, 256], P(('row', 'col')), may hold values from -6 to 6
- prior_solution: bfloat16 [16384, 256], P('col'), may hold values from -6 to 6
- factor_codes: bfloat16 [8192, 16384], P('row', 'col'), may hold values from -0.046875 to 0.046875
- block_scale: float32 [4, 64], P('row', 'col'), may hold values from 0.3 to 3
- diag_inverse: bfloat16 [4, 2048, 2048], P('row', 'col'), may hold values from -0.125 to 0.125
- inner_factor: bfloat16 [4, 4, 2048, 2048], P('row', None, 'col'), may hold values from -0.125 to 0.125
Outputs:
- solved: float32 [8192, 256], P(('row', 'col'))
All inputs are finite; a program needn't handle non-finite values.
Results may differ from a plain program's by a relative error of at most 0.0095.
Values may be sent and summed in bfloat16 or wider, within the bound.
No kernel may reach another device: no remote copies, remote signals or barrier semaphores. Data moves between devices by JAX's collectives and lax.ppermute only.
A program may use at most 64 MiB of HBM per device.

v0:
```python
import jax
import jax.numpy as jnp
from jax import lax
from jax.experimental import pallas as pl
from jax.experimental.pallas import tpu as pltpu
from jax.sharding import Mesh, PartitionSpec as P

AXES = ("cz", "cy", "rx", "rc")


def solution(mesh):
    cols, rows = mesh.shape["col"], mesh.shape["row"]
    sizes = (cols // 2, 2, rows // 2, 2)
    grid = Mesh(mesh.devices.reshape(sizes), AXES)
    count_z, _, count_x, _ = sizes
    bf16 = jnp.bfloat16

    def place(z, y, x, c):
        return ((z * 2 + y) * sizes[2] + x) * 2 + c

    def send(value, target, only=None):
        pairs = []
        for z in range(sizes[0]):
            for y in range(2):
                for x in range(sizes[2]):
                    for c in range(2):
                        if only is None or only(z, y, x, c):
                            pairs.append((place(z, y, x, c), place(*target(z, y, x, c))))
        return lax.ppermute(value, AXES, pairs)

    def over_y(z, y, x, c):
        return z, 1 - y, x, c

    def over_core(z, y, x, c):
        return z, y, x, 1 - c

    def over_both(z, y, x, c):
        return z, 1 - y, x, 1 - c

    def picked(flag, why, vectors, own, own_y, other, other_y, first):
        count = len(vectors)
        part, depth = vectors[0].shape
        each = own.shape[1]

        def kernel(flags, *refs):
            vector_refs = refs[:count]
            own_ref, own_y_ref, other_ref, other_y_ref, out_ref, held, sems = refs[count:]

            def copies(near, far):
                return [
                    pltpu.make_async_copy(
                        ref.at[first + index], held.at[2 * index + side], sems.at[2 * index + side]
                    )
                    for index in range(count)
                    for side, ref in enumerate((near, far))
                ]

            @pl.when(flags[0] == 0)
            def _():
                for copy in copies(own_ref, own_y_ref):
                    copy.start()

            @pl.when(flags[0] != 0)
            def _():
                for copy in copies(other_ref, other_y_ref):
                    copy.start()

            results = [0.0, 0.0]
            for slot, copy in enumerate(copies(own_ref, own_y_ref)):
                copy.wait()
                results[slot % 2] += lax.dot_general(
                    held[slot], vector_refs[slot // 2][...], (((1,), (1,)), ((), ())),
                    preferred_element_type=jnp.float32,
                )
            results = [value.T for value in results]
            straight = flags[1] == 0
            out_ref[:, :each] = jnp.where(straight, results[0], results[1])
            out_ref[:, each:] = jnp.where(straight, results[1], results[0])

        whole = pl.BlockSpec(memory_space=pltpu.VMEM)
        far = pl.BlockSpec(memory_space=pl.ANY)
        return pl.pallas_call(
            kernel,
            in_specs=[pl.BlockSpec(memory_space=pltpu.SMEM)] + [whole] * count + [far] * 4,
            out_specs=whole,
            scratch_shapes=[
                pltpu.VMEM((2 * count, each, depth), bf16),
                pltpu.SemaphoreType.DMA((2 * count,)),
            ],
            out_shape=jax.ShapeDtypeStruct((part, 2 * each), jnp.float32),
            cost_estimate=pl.CostEstimate(
                flops=4 * count * part * depth * each,
                bytes_accessed=4 * count * each * depth,
                transcendentals=0,
            ),
            compiler_params=pltpu.CompilerParams(vmem_limit_bytes=(4 + 4 * count) * 1024 * 1024),
        )(jnp.stack([flag, why]).astype(jnp.int32), *vectors, own, own_y, other, other_y)

    def prior_parts(zed, why, right_side, prior_solution, factor_codes, block_scale):
        each, width = right_side.shape
        panel, depth = factor_codes.shape
        blocks = block_scale.shape[1]
        deep = depth // blocks
        chunk = 2 * each

        def kernel(place_ref, scale_ref, right_ref, prior_ref, codes_ref, out_ref, scaled, total):
            step = pl.program_id(0)

            @pl.when(step == 0)
            def _():
                for b in range(blocks):
                    part = prior_ref[b * deep : (b + 1) * deep, :].astype(jnp.float32)
                    scaled[b * deep : (b + 1) * deep, :] = (part * scale_ref[0, b]).astype(bf16)

            total[...] = -jnp.dot(
                codes_ref[...], scaled[...], preferred_element_type=jnp.float32
            )

            @pl.when(step == place_ref[0])
            def _():
                rows = pl.ds(pl.multiple_of(place_ref[1] * each, each), each)
                total[rows, :] += right_ref[...]

            out_ref[0] = total[...].T.astype(bf16)

        return pl.pallas_call(
            kernel,
            grid_spec=pltpu.PrefetchScalarGridSpec(
                num_scalar_prefetch=1,
                grid=(panel // chunk,),
                in_specs=[
                    pl.BlockSpec(memory_space=pltpu.SMEM),
                    pl.BlockSpec((each, width), lambda i, p: (0, 0)),
                    pl.BlockSpec((depth, width), lambda i, p: (0, 0)),
                    pl.BlockSpec((chunk, depth), lambda i, p: (i, 0)),
                ],
                out_specs=pl.BlockSpec((1, width, chunk), lambda i, p: (i, 0, 0)),
                scratch_shapes=[
                    pltpu.VMEM((depth, width), bf16),
                    pltpu.VMEM((chunk, width), jnp.float32),
                ],
            ),
            out_shape=jax.ShapeDtypeStruct((panel // chunk, width, chunk), bf16),
            cost_estimate=pl.CostEstimate(
                flops=2 * panel * depth * width,
                bytes_accessed=2 * panel * depth + 4 * panel * width,
                transcendentals=0,
            ),
            compiler_params=pltpu.CompilerParams(vmem_limit_bytes=60 * 1024 * 1024),
        )(jnp.stack([zed, why]).astype(jnp.int32), block_scale, right_side, prior_solution, factor_codes)

    def local(right_side, prior_solution, factor_codes, block_scale, diag_inverse, inner_factor):
        each, width = right_side.shape
        part = width // 4
        zed, why = lax.axis_index("cz"), lax.axis_index("cy")
        ex, core = lax.axis_index("rx"), lax.axis_index("rc")
        chunk = 2 * each
        panel = factor_codes.shape[0]

        def gather(piece, swap=None):
            def flip(x):
                return x if swap is None else swap[::-1][swap.index(x)] if x in swap else x

            if count_z > 4:
                if swap is not None:
                    piece = send(piece, lambda z, y, x, c: (z, y, flip(x), c))
                return jnp.moveaxis(lax.all_gather(piece, "cz", axis=0), 0, 1).reshape(part, panel)
            whole = jnp.zeros((part, panel), piece.dtype)
            got = [(zed, piece)] if swap is None else []
            for step in range(1 if swap is None else 0, count_z):

                def along(z, y, x, c):
                    return (z + step) % count_z, y, flip(x), c

                moved = send(piece, along)
                got.append((lax.rem(zed + count_z - step, count_z), moved))
            for source, value in got:
                whole = lax.dynamic_update_slice(whole, value, (0, source * chunk))
            return whole

        def apply(pieces, vector):
            mine, beside = [
                lax.dot_general(
                    vector, piece, (((1,), (1,)), ((), ())), preferred_element_type=jnp.float32
                )
                for piece in pieces
            ]
            first = jnp.where(why == 0, mine, beside)
            second = jnp.where(why == 0, beside, mine)
            return jnp.concatenate([first, second], axis=1)

        def again(value):
            return jnp.where(ex < count_x, value, -value)

        def pick(even, odd):
            return lax.optimization_barrier(jnp.where(core == 0, even, odd))

        before = 2 * (count_x - 1)
        inverse = diag_inverse[0]
        turns = range(count_x)

        def inverse_at(turn):
            if turn == 0:
                return lambda z, y, x, c: x == 0 or c == 0
            return lambda z, y, x, c: x == turn and c == 1

        def odd_at(turn):
            return lambda z, y, x, c: x == turn and c == 1

        past = inner_factor[0, :before]
        past_y = send(past, over_y, lambda z, y, x, c: x > 0)
        pair = lax.dynamic_index_in_dim(inner_factor[0], 2 * ex, 0, keepdims=False)
        inverse_c = send(inverse, over_core)
        pair_c = send(pair, over_core)
        past_c = send(past, over_core)
        past_yc = send(past_y, over_core)
        pair_y, pair_yc, inverse_y, inverse_yc = {}, {}, {}, {}
        for turn in turns:
            inverse_y[turn] = send(inverse, over_y, inverse_at(turn))
            inverse_yc[turn] = send(inverse_y[turn], over_core)
            pair_y[turn] = send(pair, over_y, odd_at(turn))
            pair_yc[turn] = send(pair_y[turn], over_core)
        near_even, near_odd = pick(inverse, inverse_c), pick(inverse_c, inverse)
        near_link = pick(pair_c, pair)
        inv_even = (near_even, pick(inverse_y[0], inverse_yc[0]))
        link, inv_odd = {}, {}
        for turn in turns:
            inv_odd[turn] = (near_odd, pick(inverse_yc[turn], inverse_y[turn]))
            link[turn] = (near_link, pick(pair_yc[turn], pair_y[turn]))

        parts = prior_parts(zed, why, right_side, prior_solution, factor_codes, block_scale)
        parts = parts.reshape(count_z * 4, part, chunk)
        came = lax.all_to_all(parts, ("cz", "cy", "rc"), 0, 0)
        came = came.reshape(count_z * 2, 2, part, chunk)
        rhs_even = came[:, 0].astype(jnp.float32).sum(0)
        came, rhs_even = lax.optimization_barrier((came, rhs_even))
        rhs_odd = came[:, 1].astype(jnp.float32).sum(0)

        kept = (None, None)
        for turn in turns:
            vector = gather(rhs_even.astype(bf16))
            even = apply(inv_even, vector)
            even_all = gather(even.astype(bf16))
            current = rhs_odd - apply(link[turn], even_all)
            vector = gather(current.astype(bf16))
            odd = apply(inv_odd[turn], vector)
            kept = [
                new if turn == 0 else jnp.where(ex == turn, new, old)
                for new, old in zip((even, odd), kept)
            ]
            for later in range(turn + 1, count_x):

                def exchange(z, y, x, c):
                    return z, y, later if x == turn else turn if x == later else x, c

                seen_even = send(again(even_all), exchange)
                seen_odd = gather(odd.astype(bf16), [turn, later])
                here = ex == later
                add = picked(core, why, [seen_even], past, past_y, past_c, past_yc, 2 * turn)
                near = pick(past[2 * turn + 1], past_c[2 * turn + 1])
                far = pick(past_y[2 * turn + 1], past_yc[2 * turn + 1])
                add = add + apply((near, far), seen_odd)
                rhs_even = rhs_even - jnp.where(here, add, 0.0)
                seen = [seen_even, again(seen_odd)]
                add = picked(
                    1 - core, why, seen, past, past_y, past_c, past_yc, 2 * turn
                )
                rhs_odd = rhs_odd - jnp.where(here, add, 0.0)

        near = [jnp.where(why == 0, v[:, :each], v[:, each:]) for v in kept]
        far = [jnp.where(why == 0, v[:, each:], v[:, :each]) for v in kept]
        mine = jnp.where(core == 0, near[0], near[1])
        from_y = send(jnp.where(core == 0, far[0], far[1]).astype(bf16), over_y)
        from_yc = send(jnp.where(core == 0, far[1], far[0]).astype(bf16), over_both)
        from_c = send(jnp.where(core == 0, near[1], near[0]), over_core)
        from_y, from_yc = from_y.astype(jnp.float32), from_yc.astype(jnp.float32)
        by_y = [
            (jnp.where(core == 0, v, w), jnp.where(core == 0, w, v))
            for v, w in ((mine, from_c), (from_y, from_yc))
        ]
        blocks_out = [jnp.where(why == 0, v, w) for v, w in zip(by_y[0], by_y[1])]
        blocks_out += [jnp.where(why == 0, w, v) for v, w in zip(by_y[0], by_y[1])]
        return jnp.concatenate(blocks_out, axis=0).T

    return jax.shard_map(
        local,
        mesh=grid,
        in_specs=(
            P(("rx", "rc", "cz", "cy"), None),
            P(("cz", "cy"), None),
            P(("rx", "rc"), ("cz", "cy")),
            P(("rx", "rc"), ("cz", "cy")),
            P(("rx", "rc"), ("cz", "cy"), None),
            P(("rx", "rc"), None, ("cz", "cy"), None),
        ),
        out_specs=P(("rx", "rc", "cz", "cy"), None),
        check_vma=False,
    )
```

profile of v0, /device:TPU:0, one launch (start us, length us, event | category | flops | bytes accessed | tf_op | source)
XLA Modules:
  0.0 182.3 jit_solution(13287262876716370891)
XLA Ops:
  0.0 0.6 pad_add_fusion.place_ref
  0.6 8.0 %shard_map.64 = bf16[4,256,512]{2,1,0:T(8,128)(2,1)} custom-call(s32[2]{0:T(128)} %pad_add_fusion.place_ref, f32[1,8]{1,0:T(1,128)} %scale_ref.1, f32[256,256]{1,0:T(8,128)} %right_ref.1, bf16[2048,256]{1,0:T(8,128)(2,1)} %prior_ref.1, bf16[2048,2048]{1,0:T(8,128)(2,1)} %codes_ref.1), custom_call_target="tpu_custom_call" | custom-call | flops 2147483648 | bytes 10485760 | tf_op jit(solution)/shard_map/pallas_call | solution.py:126
  8.6 7.4 %all-to-all-start = ((bf16[16,64,512]{2,1,0:T(8,128)(2,1)}), bf16[16,64,512]{2,1,0:T(8,128)(2,1)S(1)}, u32[]{:S(2)}, u32[]{:S(2)}) async-start(bf16[16,64,512]{2,1,0:T(8,128)(2,1)} %bitcast.55), calls=%async_computation | async-start | bytes 2097152 | tf_op jit(solution)/shard_map/all_to_all | solution.py:233
  16.0 3.8 %collective-permute-start.4 = (bf16[256,2048]{1,0:T(8,128)(2,1)}, bf16[256,2048]{1,0:T(8,128)(2,1)}, u32[]{:S(2)}, u32[]{:S(2)}) collective-permute-start(bf16[256,2048]{1,0:T(8,128)(2,1)} %bitcast.5), channel_id=1, source_target_pairs={{0,4},{1,5},{2,6},{4,0},{5,1},{6,2},{8,12},{9,13},{10,14},{12,8},{... | collective-permute-start | bytes 3145736 | tf_op jit(solution)/shard_map/ppermute | solution.py:29
  19.9 2.3 %dynamic-slice_bitcast_fusion = bf16[256,2048]{1,0:T(8,128)(2,1)} fusion(bf16[1,4,256,2048]{3,2,1,0:T(8,128)(2,1)} %param.11, s32[]{:T(128)S(6)} %select_n.265), kind=kLoop, calls=%fused_computation.5 | loop fusion | bytes 2097156 | tf_op jit(solution)/shard_map/jit(dynamic_index_in_dim)/squeeze | solution.py:212
  22.2 1.6 collective-permute-start.14
  23.9 0.8 collective-permute-start.13
  24.8 1.7 slice_bitcast_fusion.refs_1_.refs_2_
  26.5 12.4 %all-to-all-done = bf16[16,64,512]{2,1,0:T(8,128)(2,1)S(1)} async-done(((bf16[16,64,512]{2,1,0:T(8,128)(2,1)}), bf16[16,64,512]{2,1,0:T(8,128)(2,1)S(1)}, u32[]{:S(2)}, u32[]{:S(2)}) %all-to-all-start) | async-done | bytes 1048608 | tf_op jit(solution)/shard_map/all_to_all | solution.py:233
  39.0 3.3 %collective-permute-start = (bf16[64,512]{1,0:T(8,128)(2,1)S(1)}, bf16[64,512]{1,0:T(8,128)(2,1)S(1)}, u32[]{:S(2)}, u32[]{:S(2)}) collective-permute-start(bf16[64,512]{1,0:T(8,128)(2,1)S(1)} %get-tuple-element.23), channel_id=1, source_target_pairs={{0,8},{1,9},{2,10},{3,11},{4,12},{5,13},{6,14},{7,15},{8,16},{9,17... | collective-permute-start | bytes 196616 | tf_op jit(solution)/shard_map/ppermute | solution.py:29
  42.4 11.1 %collective-permute-done.4 = bf16[256,2048]{1,0:T(8,128)(2,1)} collective-permute-done((bf16[256,2048]{1,0:T(8,128)(2,1)}, bf16[256,2048]{1,0:T(8,128)(2,1)}, u32[]{:S(2)}, u32[]{:S(2)}) %collective-permute-start.4) | collective-permute-done | bytes 1048608 | tf_op jit(solution)/shard_map/ppermute | solution.py:29
  53.5 0.7 collective-permute-start.29
  54.2 0.7 collective-permute-start.34
  55.1 2.4 %collective-permute-start.1 = (bf16[64,512]{1,0:T(8,128)(2,1)S(1)}, bf16[64,512]{1,0:T(8,128)(2,1)S(1)}, u32[]{:S(2)}, u32[]{:S(2)}) collective-permute-start(bf16[64,512]{1,0:T(8,128)(2,1)S(1)} %get-tuple-element.23), channel_id=1, source_target_pairs={{0,16},{1,17},{2,18},{3,19},{4,20},{5,21},{6,22},{7,23},{8,24},{9,... | collective-permute-start | bytes 196616 | tf_op jit(solution)/shard_map/ppermute | solution.py:29
  57.5 1.7 broadcast_select_fusion.3
  59.2 2.7 %collective-permute-done.1 = bf16[64,512]{1,0:T(8,128)(2,1)S(1)} collective-permute-done((bf16[64,512]{1,0:T(8,128)(2,1)S(1)}, bf16[64,512]{1,0:T(8,128)(2,1)S(1)}, u32[]{:S(2)}, u32[]{:S(2)}) %collective-permute-start.1) | collective-permute-done | bytes 65568 | tf_op jit(solution)/shard_map/ppermute | solution.py:29
  61.9 3.3 %collective-permute-start.2 = (bf16[64,512]{1,0:T(8,128)(2,1)S(1)}, bf16[64,512]{1,0:T(8,128)(2,1)S(1)}, u32[]{:S(2)}, u32[]{:S(2)}) collective-permute-start(bf16[64,512]{1,0:T(8,128)(2,1)S(1)} %get-tuple-element.23), channel_id=1, source_target_pairs={{0,24},{1,25},{2,26},{3,27},{4,28},{5,29},{6,30},{7,31},{8,0},{9,1... | collective-permute-start | bytes 196616 | tf_op jit(solution)/shard_map/ppermute | solution.py:29
  65.1 1.4 broadcast_select_fusion.5
  66.5 0.5 collective-permute-done.2
  67.2 0.8 collective-permute-start.10
  68.0 0.6 collective-permute-start.15
  69.1 1.5 broadcast_select_fusion.2
  71.0 0.5 broadcast_select_fusion.25
  71.5 1.2 collective-permute-done.15
  72.8 4.8 %collective-permute-start.7 = (bf16[64,512]{1,0:T(8,128)(2,1)S(1)}, bf16[64,512]{1,0:T(8,128)(2,1)S(1)}, u32[]{:S(2)}, u32[]{:S(2)}) collective-permute-start(bf16[64,512]{1,0:T(8,128)(2,1)S(1)} %get-tuple-element.21), channel_id=1, source_target_pairs={{0,16},{1,17},{2,18},{3,19},{4,20},{5,21},{6,22},{7,23},{8,24},{9,... | collective-permute-start | bytes 196616 | tf_op jit(solution)/shard_map/ppermute | solution.py:29
  77.8 1.4 collective-permute-done.6
  79.3 2.8 %collective-permute-done.7 = bf16[64,512]{1,0:T(8,128)(2,1)S(1)} collective-permute-done((bf16[64,512]{1,0:T(8,128)(2,1)S(1)}, bf16[64,512]{1,0:T(8,128)(2,1)S(1)}, u32[]{:S(2)}, u32[]{:S(2)}) %collective-permute-start.7) | collective-permute-done | bytes 65568 | tf_op jit(solution)/shard_map/ppermute | solution.py:29
  82.1 1.3 collective-permute-done.8
  83.9 0.5 broadcast_select_fusion.23
  84.4 0.6 collective-permute-start.16
  85.1 2.4 %collective-permute-start.17 = (bf16[64,512]{1,0:T(8,128)(2,1)S(1)}, bf16[64,512]{1,0:T(8,128)(2,1)S(1)}, u32[]{:S(2)}, u32[]{:S(2)}) collective-permute-start(bf16[64,512]{1,0:T(8,128)(2,1)S(1)} %get-tuple-element.19), channel_id=1, source_target_pairs={{0,16},{1,17},{2,18},{3,19},{4,20},{5,21},{6,22},{7,23},{8,24},{9,... | collective-permute-start | bytes 196616 | tf_op jit(solution)/shard_map/ppermute | solution.py:29
  87.5 1.1 collective-permute-start.18
  88.5 2.7 %collective-permute-done.16 = bf16[64,512]{1,0:T(8,128)(2,1)S(1)} collective-permute-done((bf16[64,512]{1,0:T(8,128)(2,1)S(1)}, bf16[64,512]{1,0:T(8,128)(2,1)S(1)}, u32[]{:S(2)}, u32[]{:S(2)}) %collective-permute-start.16) | collective-permute-done | bytes 65568 | tf_op jit(solution)/shard_map/ppermute | solution.py:29
  91.3 2.0 %collective-permute-done.17 = bf16[64,512]{1,0:T(8,128)(2,1)S(1)} collective-permute-done((bf16[64,512]{1,0:T(8,128)(2,1)S(1)}, bf16[64,512]{1,0:T(8,128)(2,1)S(1)}, u32[]{:S(2)}, u32[]{:S(2)}) %collective-permute-start.17) | collective-permute-done | bytes 65568 | tf_op jit(solution)/shard_map/ppermute | solution.py:29
  94.2 35.3 %collective-permute-start.19 = (bf16[64,512]{1,0:T(8,128)(2,1)S(1)}, bf16[64,512]{1,0:T(8,128)(2,1)S(1)}, u32[]{:S(2)}, u32[]{:S(2)}) collective-permute-start(bf16[64,512]{1,0:T(8,128)(2,1)S(1)} %fusion.9), channel_id=1, source_target_pairs={{0,2},{1,3},{2,0},{3,1},{4,6},{5,7},{6,4},{7,5},{8,10},{9,11},{10,... | collective-permute-start | bytes 196616 | tf_op jit(solution)/shard_map/ppermute | solution.py:29
  129.6 2.6 %collective-permute-start.20 = (bf16[64,512]{1,0:T(8,128)(2,1)S(1)}, bf16[64,512]{1,0:T(8,128)(2,1)S(1)}, u32[]{:S(2)}, u32[]{:S(2)}) collective-permute-start(bf16[64,512]{1,0:T(8,128)(2,1)S(1)} %fusion.9), channel_id=1, source_target_pairs={{0,10},{1,11},{2,8},{3,9},{4,14},{5,15},{6,12},{7,13},{8,18},{9,19... | collective-permute-start | bytes 196616 | tf_op jit(solution)/shard_map/ppermute | solution.py:29
  132.2 1.8 collective-permute-start.21
  134.1 2.9 %collective-permute-done.20 = bf16[64,512]{1,0:T(8,128)(2,1)S(1)} collective-permute-done((bf16[64,512]{1,0:T(8,128)(2,1)S(1)}, bf16[64,512]{1,0:T(8,128)(2,1)S(1)}, u32[]{:S(2)}, u32[]{:S(2)}) %collective-permute-start.20) | collective-permute-done | bytes 65568 | tf_op jit(solution)/shard_map/ppermute | solution.py:29
  136.9 0.9 collective-permute-start.22
  137.9 1.8 collective-permute-done.21
  139.7 2.4 %collective-permute-done.22 = bf16[64,512]{1,0:T(8,128)(2,1)S(1)} collective-permute-done((bf16[64,512]{1,0:T(8,128)(2,1)S(1)}, bf16[64,512]{1,0:T(8,128)(2,1)S(1)}, u32[]{:S(2)}, u32[]{:S(2)}) %collective-permute-start.22) | collective-permute-done | bytes 65568 | tf_op jit(solution)/shard_map/ppermute | solution.py:29
  142.3 2.1 %shard_map.65 = f32[64,512]{1,0:T(8,128)S(1)} custom-call(s32[2]{0:T(128)S(1)} %pad_add_fusion.1.flags, bf16[64,2048]{1,0:T(8,128)(2,1)S(1)} %collective-permute-done.9.refs_0_, bf16[2,256,2048]{2,1,0:T(8,128)(2,1)S(1)} %slice_bitcast_fusion.refs_1_.refs_2_, bf16[2,256,2048]{2,1,0:T(8,128)(2,1)S(1)} %collective-permute-done.10.refs_2_.refs_3_, ...), custom_call_target="tpu_custom_call" | custom-call | flops 134217728 | bytes 2097152 | tf_op jit(solution)/shard_map/pallas_call | solution.py:82
  145.3 0.8 collective-permute-start.23
  146.2 2.6 %collective-permute-start.24 = (bf16[64,512]{1,0:T(8,128)(2,1)S(1)}, bf16[64,512]{1,0:T(8,128)(2,1)S(1)}, u32[]{:S(2)}, u32[]{:S(2)}) collective-permute-start(bf16[64,512]{1,0:T(8,128)(2,1)S(1)} %get-tuple-element.17), channel_id=1, source_target_pairs={{0,16},{1,17},{2,18},{3,19},{4,20},{5,21},{6,22},{7,23},{8,24},{9,... | collective-permute-start | bytes 196616 | tf_op jit(solution)/shard_map/ppermute | solution.py:29
  148.9 0.6 collective-permute-start.25
  149.5 2.1 %collective-permute-done.23 = bf16[64,512]{1,0:T(8,128)(2,1)S(1)} collective-permute-done((bf16[64,512]{1,0:T(8,128)(2,1)S(1)}, bf16[64,512]{1,0:T(8,128)(2,1)S(1)}, u32[]{:S(2)}, u32[]{:S(2)}) %collective-permute-start.23) | collective-permute-done | bytes 65568 | tf_op jit(solution)/shard_map/ppermute | solution.py:29
  151.6 1.3 collective-permute-done.24
  152.9 0.6 collective-permute-done.25
  154.5 0.7 collective-permute-start.26
  155.3 3.5 %shard_map.66 = f32[64,512]{1,0:T(8,128)S(1)} custom-call(s32[2]{0:T(128)S(1)} %pad_add_fusion.2.flags, bf16[64,2048]{1,0:T(8,128)(2,1)S(1)} %collective-permute-done.9.refs_0_, bf16[64,2048]{1,0:T(8,128)(2,1)S(1)} %negate_select_fusion.refs_1_, bf16[2,256,2048]{2,1,0:T(8,128)(2,1)S(1)} %slice_bitcast_fusion.refs_1_.refs_2_, ...), custom_call_target="tpu_custom_call" | custom-call | flops 268435456 | bytes 4194304 | tf_op jit(solution)/shard_map/pallas_call | solution.py:82
  158.8 2.4 %collective-permute-start.27 = (bf16[64,512]{1,0:T(8,128)(2,1)S(1)}, bf16[64,512]{1,0:T(8,128)(2,1)S(1)}, u32[]{:S(2)}, u32[]{:S(2)}) collective-permute-start(bf16[64,512]{1,0:T(8,128)(2,1)S(1)} %get-tuple-element.15), channel_id=1, source_target_pairs={{0,16},{1,17},{2,18},{3,19},{4,20},{5,21},{6,22},{7,23},{8,24},{9,... | collective-permute-start | bytes 196616 | tf_op jit(solution)/shard_map/ppermute | solution.py:29
  161.2 0.9 collective-permute-start.28
  162.1 2.6 %collective-permute-done.27 = bf16[64,512]{1,0:T(8,128)(2,1)S(1)} collective-permute-done((bf16[64,512]{1,0:T(8,128)(2,1)S(1)}, bf16[64,512]{1,0:T(8,128)(2,1)S(1)}, u32[]{:S(2)}, u32[]{:S(2)}) %collective-permute-start.27) | collective-permute-done | bytes 65568 | tf_op jit(solution)/shard_map/ppermute | solution.py:29
  164.7 0.7 collective-permute-done.28
  165.9 0.5 broadcast_select_fusion.15
  166.4 1.4 collective-permute-start.31
  167.9 2.9 %collective-permute-start.32 = (bf16[64,512]{1,0:T(8,128)(2,1)S(1)}, bf16[64,512]{1,0:T(8,128)(2,1)S(1)}, u32[]{:S(2)}, u32[]{:S(2)}) collective-permute-start(bf16[64,512]{1,0:T(8,128)(2,1)S(1)} %get-tuple-element.13), channel_id=1, source_target_pairs={{0,16},{1,17},{2,18},{3,19},{4,20},{5,21},{6,22},{7,23},{8,24},{9,... | collective-permute-start | bytes 196616 | tf_op jit(solution)/shard_map/ppermute | solution.py:29
  170.8 1.8 collective-permute-done.31
  172.6 1.4 collective-permute-done.32
  174.0 1.1 collective-permute-done.33
  176.1 1.9 %collective-permute-start.37 = (bf16[64,256]{1,0:T(8,128)(2,1)S(1)}, bf16[64,256]{1,0:T(8,128)(2,1)S(1)}, u32[]{:S(2)}, u32[]{:S(2)}) collective-permute-start(bf16[64,256]{1,0:T(8,128)(2,1)S(1)} %get-tuple-element.33), channel_id=1, source_target_pairs={{0,4},{1,5},{2,6},{3,7},{4,0},{5,1},{6,2},{7,3},{8,12},{9,13},{10,... | collective-permute-start | bytes 98312 | tf_op jit(solution)/shard_map/ppermute | solution.py:29
  178.2 1.9 %collective-permute-done.37 = bf16[64,256]{1,0:T(8,128)(2,1)S(1)} collective-permute-done((bf16[64,256]{1,0:T(8,128)(2,1)S(1)}, bf16[64,256]{1,0:T(8,128)(2,1)S(1)}, u32[]{:S(2)}, u32[]{:S(2)}) %collective-permute-start.37) | collective-permute-done | bytes 32800 | tf_op jit(solution)/shard_map/ppermute | solution.py:29
  180.1 1.3 collective-permute-done.38
  181.4 0.8 copy.7
  (95 shorter events, 7.6 us)
Async XLA Ops:
  8.6 30.3 %all-to-all-start = ((bf16[16,64,512]{2,1,0:T(8,128)(2,1)}), bf16[16,64,512]{2,1,0:T(8,128)(2,1)S(1)}, u32[]{:S(2)}, u32[]{:S(2)}) async-start(bf16[16,64,512]{2,1,0:T(8,128)(2,1)} %bitcast.55), calls=%async_computation | async-start | bytes 2097152 | tf_op jit(solution)/shard_map/all_to_all | solution.py:233
  16.0 37.5 %collective-permute-start.4 = (bf16[256,2048]{1,0:T(8,128)(2,1)}, bf16[256,2048]{1,0:T(8,128)(2,1)}, u32[]{:S(2)}, u32[]{:S(2)}) collective-permute-start(bf16[256,2048]{1,0:T(8,128)(2,1)} %bitcast.5), channel_id=1, source_target_pairs={{0,4},{1,5},{2,6},{4,0},{5,1},{6,2},{8,12},{9,13},{10,14},{12,8},{... | collective-permute-start | bytes 3145736 | tf_op jit(solution)/shard_map/ppermute | solution.py:29
  19.8 34.4 %collective-permute-start.3 = (bf16[256,2048]{1,0:T(8,128)(2,1)}, bf16[256,2048]{1,0:T(8,128)(2,1)}, u32[]{:S(2)}, u32[]{:S(2)}) collective-permute-start(bf16[256,2048]{1,0:T(8,128)(2,1)} %bitcast.5), channel_id=1, source_target_pairs={{0,1},{1,0},{2,3},{3,2},{4,5},{5,4},{6,7},{7,6},{8,9},{9,8},{10,11... | collective-permute-start | bytes 3145736 | tf_op jit(solution)/shard_map/ppermute | solution.py:29
  22.2 44.9 %collective-permute-start.14 = (bf16[256,2048]{1,0:T(8,128)(2,1)}, bf16[256,2048]{1,0:T(8,128)(2,1)}, u32[]{:S(2)}, u32[]{:S(2)}) collective-permute-start(bf16[256,2048]{1,0:T(8,128)(2,1)} %dynamic-slice_bitcast_fusion), channel_id=1, source_target_pairs={{1,5},{5,1},{9,13},{13,9},{17,21},{21,17},{25,29},{29,25}} | collective-permute-start | bytes 3145736 | tf_op jit(solution)/shard_map/ppermute | solution.py:29
  23.9 31.1 %collective-permute-start.13 = (bf16[256,2048]{1,0:T(8,128)(2,1)}, bf16[256,2048]{1,0:T(8,128)(2,1)}, u32[]{:S(2)}, u32[]{:S(2)}) collective-permute-start(bf16[256,2048]{1,0:T(8,128)(2,1)} %dynamic-slice_bitcast_fusion), channel_id=1, source_target_pairs={{0,1},{1,0},{2,3},{3,2},{4,5},{5,4},{6,7},{7,6},{8,9},{9,8},{10,11... | collective-permute-start | bytes 3145736 | tf_op jit(solution)/shard_map/ppermute | solution.py:29
  39.0 16.0 %collective-permute-start = (bf16[64,512]{1,0:T(8,128)(2,1)S(1)}, bf16[64,512]{1,0:T(8,128)(2,1)S(1)}, u32[]{:S(2)}, u32[]{:S(2)}) collective-permute-start(bf16[64,512]{1,0:T(8,128)(2,1)S(1)} %get-tuple-element.23), channel_id=1, source_target_pairs={{0,8},{1,9},{2,10},{3,11},{4,12},{5,13},{6,14},{7,15},{8,16},{9,17... | collective-permute-start | bytes 196616 | tf_op jit(solution)/shard_map/ppermute | solution.py:29
  42.4 22.8 %copy-start = (bf16[1,4,256,2048]{3,2,1,0:T(8,128)(2,1)S(1)}, bf16[1,4,256,2048]{3,2,1,0:T(8,128)(2,1)}, u32[]{:S(2)}) copy-start(bf16[1,4,256,2048]{3,2,1,0:T(8,128)(2,1)} %param.11) | copy-start | bytes 12582916
  53.5 14.5 %collective-permute-start.29 = (bf16[256,2048]{1,0:T(8,128)(2,1)}, bf16[256,2048]{1,0:T(8,128)(2,1)S(1)}, u32[]{:S(2)}, u32[]{:S(2)}) collective-permute-start(bf16[256,2048]{1,0:T(8,128)(2,1)} %dynamic-slice_bitcast_fusion), channel_id=1, source_target_pairs={{3,7},{7,3},{11,15},{15,11},{19,23},{23,19},{27,31},{31,27}} | collective-permute-start | bytes 3145736 | tf_op jit(solution)/shard_map/ppermute | solution.py:29
  54.2 14.3 %collective-permute-start.34 = (bf16[256,2048]{1,0:T(8,128)(2,1)}, bf16[256,2048]{1,0:T(8,128)(2,1)S(1)}, u32[]{:S(2)}, u32[]{:S(2)}) collective-permute-start(bf16[256,2048]{1,0:T(8,128)(2,1)} %bitcast.5), channel_id=1, source_target_pairs={{3,7},{7,3},{11,15},{15,11},{19,23},{23,19},{27,31},{31,27}} | collective-permute-start | bytes 3145736 | tf_op jit(solution)/shard_map/ppermute | solution.py:29
  55.0 13.7 %collective-permute-start.5 = (bf16[256,2048]{1,0:T(8,128)(2,1)}, bf16[256,2048]{1,0:T(8,128)(2,1)S(1)}, u32[]{:S(2)}, u32[]{:S(2)}) collective-permute-start(bf16[256,2048]{1,0:T(8,128)(2,1)} %collective-permute-done.4), channel_id=1, source_target_pairs={{0,1},{1,0},{2,3},{3,2},{4,5},{5,4},{6,7},{7,6},{8,9},{9,8},{10,11... | collective-permute-start | bytes 3145736 | tf_op jit(solution)/shard_map/ppermute | solution.py:29
  55.1 6.8 %collective-permute-start.1 = (bf16[64,512]{1,0:T(8,128)(2,1)S(1)}, bf16[64,512]{1,0:T(8,128)(2,1)S(1)}, u32[]{:S(2)}, u32[]{:S(2)}) collective-permute-start(bf16[64,512]{1,0:T(8,128)(2,1)S(1)} %get-tuple-element.23), channel_id=1, source_target_pairs={{0,16},{1,17},{2,18},{3,19},{4,20},{5,21},{6,22},{7,23},{8,24},{9,... | collective-permute-start | bytes 196616 | tf_op jit(solution)/shard_map/ppermute | solution.py:29
  61.9 5.2 %collective-permute-start.2 = (bf16[64,512]{1,0:T(8,128)(2,1)S(1)}, bf16[64,512]{1,0:T(8,128)(2,1)S(1)}, u32[]{:S(2)}, u32[]{:S(2)}) collective-permute-start(bf16[64,512]{1,0:T(8,128)(2,1)S(1)} %get-tuple-element.23), channel_id=1, source_target_pairs={{0,24},{1,25},{2,26},{3,27},{4,28},{5,29},{6,30},{7,31},{8,0},{9,1... | collective-permute-start | bytes 196616 | tf_op jit(solution)/shard_map/ppermute | solution.py:29
  67.0 5.8 %collective-permute-start.11 = (bf16[2,256,2048]{2,1,0:T(8,128)(2,1)S(1)}, bf16[2,256,2048]{2,1,0:T(8,128)(2,1)S(1)}, u32[]{:S(2)}, u32[]{:S(2)}) collective-permute-start(bf16[2,256,2048]{2,1,0:T(8,128)(2,1)S(1)} %slice_bitcast_fusion.refs_1_.refs_2_), channel_id=1, source_target_pairs={{0,1},{1,0},{2,3},{3,2},{4,5},{5,4},{6,7},{7,6},{8,9},{9,8},{10,11... | collective-permute-start | bytes 6291464 | tf_op jit(solution)/shard_map/ppermute | solution.py:29
  67.2 10.6 %collective-permute-start.10 = (bf16[2,256,2048]{2,1,0:T(8,128)(2,1)S(1)}, bf16[2,256,2048]{2,1,0:T(8,128)(2,1)S(1)}, u32[]{:S(2)}, u32[]{:S(2)}) collective-permute-start(bf16[2,256,2048]{2,1,0:T(8,128)(2,1)S(1)} %slice_bitcast_fusion.refs_1_.refs_2_), channel_id=1, source_target_pairs={{2,6},{3,7},{6,2},{7,3},{10,14},{11,15},{14,10},{15,11},{18,22},{1... | collective-permute-start | bytes 6291464 | tf_op jit(solution)/shard_map/ppermute | solution.py:29
  68.0 4.7 %collective-permute-start.15 = (bf16[256,2048]{1,0:T(8,128)(2,1)}, bf16[256,2048]{1,0:T(8,128)(2,1)S(1)}, u32[]{:S(2)}, u32[]{:S(2)}) collective-permute-start(bf16[256,2048]{1,0:T(8,128)(2,1)} %collective-permute-done.14), channel_id=1, source_target_pairs={{0,1},{1,0},{2,3},{3,2},{4,5},{5,4},{6,7},{7,6},{8,9},{9,8},{10,11... | collective-permute-start | bytes 3145736 | tf_op jit(solution)/shard_map/ppermute | solution.py:29
  68.6 16.4 %collective-permute-start.30 = (bf16[256,2048]{1,0:T(8,128)(2,1)S(1)}, bf16[256,2048]{1,0:T(8,128)(2,1)S(1)}, u32[]{:S(2)}, u32[]{:S(2)}) collective-permute-start(bf16[256,2048]{1,0:T(8,128)(2,1)S(1)} %collective-permute-done.29), channel_id=1, source_target_pairs={{0,1},{1,0},{2,3},{3,2},{4,5},{5,4},{6,7},{7,6},{8,9},{9,8},{10,11... | collective-permute-start | bytes 3145736 | tf_op jit(solution)/shard_map/ppermute | solution.py:29
  68.7 77.5 %collective-permute-start.35 = (bf16[256,2048]{1,0:T(8,128)(2,1)S(1)}, bf16[256,2048]{1,0:T(8,128)(2,1)S(1)}, u32[]{:S(2)}, u32[]{:S(2)}) collective-permute-start(bf16[256,2048]{1,0:T(8,128)(2,1)S(1)} %collective-permute-done.34), channel_id=1, source_target_pairs={{0,1},{1,0},{2,3},{3,2},{4,5},{5,4},{6,7},{7,6},{8,9},{9,8},{10,11... | collective-permute-start | bytes 3145736 | tf_op jit(solution)/shard_map/ppermute | solution.py:29
  72.7 6.6 %collective-permute-start.6 = (bf16[64,512]{1,0:T(8,128)(2,1)S(1)}, bf16[64,512]{1,0:T(8,128)(2,1)S(1)}, u32[]{:S(2)}, u32[]{:S(2)}) collective-permute-start(bf16[64,512]{1,0:T(8,128)(2,1)S(1)} %get-tuple-element.21), channel_id=1, source_target_pairs={{0,8},{1,9},{2,10},{3,11},{4,12},{5,13},{6,14},{7,15},{8,16},{9,17... | collective-permute-start | bytes 196616 | tf_op jit(solution)/shard_map/ppermute | solution.py:29
  72.8 9.2 %collective-permute-start.7 = (bf16[64,512]{1,0:T(8,128)(2,1)S(1)}, bf16[64,512]{1,0:T(8,128)(2,1)S(1)}, u32[]{:S(2)}, u32[]{:S(2)}) collective-permute-start(bf16[64,512]{1,0:T(8,128)(2,1)S(1)} %get-tuple-element.21), channel_id=1, source_target_pairs={{0,16},{1,17},{2,18},{3,19},{4,20},{5,21},{6,22},{7,23},{8,24},{9,... | collective-permute-start | bytes 196616 | tf_op jit(solution)/shard_map/ppermute | solution.py:29
  77.8 5.7 %collective-permute-start.8 = (bf16[64,512]{1,0:T(8,128)(2,1)S(1)}, bf16[64,512]{1,0:T(8,128)(2,1)S(1)}, u32[]{:S(2)}, u32[]{:S(2)}) collective-permute-start(bf16[64,512]{1,0:T(8,128)(2,1)S(1)} %get-tuple-element.21), channel_id=1, source_target_pairs={{0,24},{1,25},{2,26},{3,27},{4,28},{5,29},{6,30},{7,31},{8,0},{9,1... | collective-permute-start | bytes 196616 | tf_op jit(solution)/shard_map/ppermute | solution.py:29
  79.2 62.9 %collective-permute-start.12 = (bf16[2,256,2048]{2,1,0:T(8,128)(2,1)S(1)}, bf16[2,256,2048]{2,1,0:T(8,128)(2,1)S(1)}, u32[]{:S(2)}, u32[]{:S(2)}) collective-permute-start(bf16[2,256,2048]{2,1,0:T(8,128)(2,1)S(1)} %collective-permute-done.10.refs_2_.refs_3_), channel_id=1, source_target_pairs={{0,1},{1,0},{2,3},{3,2},{4,5},{5,4},{6,7},{7,6},{8,9},{9,8},{10,11... | collective-permute-start | bytes 6291464 | tf_op jit(solution)/shard_map/ppermute | solution.py:29
  84.4 6.9 %collective-permute-start.16 = (bf16[64,512]{1,0:T(8,128)(2,1)S(1)}, bf16[64,512]{1,0:T(8,128)(2,1)S(1)}, u32[]{:S(2)}, u32[]{:S(2)}) collective-permute-start(bf16[64,512]{1,0:T(8,128)(2,1)S(1)} %get-tuple-element.19), channel_id=1, source_target_pairs={{0,8},{1,9},{2,10},{3,11},{4,12},{5,13},{6,14},{7,15},{8,16},{9,17... | collective-permute-start | bytes 196616 | tf_op jit(solution)/shard_map/ppermute | solution.py:29
  85.1 8.2 %collective-permute-start.17 = (bf16[64,512]{1,0:T(8,128)(2,1)S(1)}, bf16[64,512]{1,0:T(8,128)(2,1)S(1)}, u32[]{:S(2)}, u32[]{:S(2)}) collective-permute-start(bf16[64,512]{1,0:T(8,128)(2,1)S(1)} %get-tuple-element.19), channel_id=1, source_target_pairs={{0,16},{1,17},{2,18},{3,19},{4,20},{5,21},{6,22},{7,23},{8,24},{9,... | collective-permute-start | bytes 196616 | tf_op jit(solution)/shard_map/ppermute | solution.py:29
  87.5 5.8 %collective-permute-start.18 = (bf16[64,512]{1,0:T(8,128)(2,1)S(1)}, bf16[64,512]{1,0:T(8,128)(2,1)S(1)}, u32[]{:S(2)}, u32[]{:S(2)}) collective-permute-start(bf16[64,512]{1,0:T(8,128)(2,1)S(1)} %get-tuple-element.19), channel_id=1, source_target_pairs={{0,24},{1,25},{2,26},{3,27},{4,28},{5,29},{6,30},{7,31},{8,0},{9,1... | collective-permute-start | bytes 196616 | tf_op jit(solution)/shard_map/ppermute | solution.py:29
  94.2 38.0 %collective-permute-start.19 = (bf16[64,512]{1,0:T(8,128)(2,1)S(1)}, bf16[64,512]{1,0:T(8,128)(2,1)S(1)}, u32[]{:S(2)}, u32[]{:S(2)}) collective-permute-start(bf16[64,512]{1,0:T(8,128)(2,1)S(1)} %fusion.9), channel_id=1, source_target_pairs={{0,2},{1,3},{2,0},{3,1},{4,6},{5,7},{6,4},{7,5},{8,10},{9,11},{10,... | collective-permute-start | bytes 196616 | tf_op jit(solution)/shard_map/ppermute | solution.py:29
  129.5 12.8 %collective-permute-start.9 = (bf16[64,2048]{1,0:T(8,128)(2,1)S(1)}, bf16[64,2048]{1,0:T(8,128)(2,1)S(1)}, u32[]{:S(2)}, u32[]{:S(2)}) collective-permute-start(bf16[64,2048]{1,0:T(8,128)(2,1)S(1)} %negate_select_fusion.1), channel_id=1, source_target_pairs={{0,2},{1,3},{2,0},{3,1},{4,6},{5,7},{6,4},{7,5},{8,10},{9,11},{10,... | collective-permute-start | bytes 786440 | tf_op jit(solution)/shard_map/ppermute | solution.py:29
  129.6 7.3 %collective-permute-start.20 = (bf16[64,512]{1,0:T(8,128)(2,1)S(1)}, bf16[64,512]{1,0:T(8,128)(2,1)S(1)}, u32[]{:S(2)}, u32[]{:S(2)}) collective-permute-start(bf16[64,512]{1,0:T(8,128)(2,1)S(1)} %fusion.9), channel_id=1, source_target_pairs={{0,10},{1,11},{2,8},{3,9},{4,14},{5,15},{6,12},{7,13},{8,18},{9,19... | collective-permute-start | bytes 196616 | tf_op jit(solution)/shard_map/ppermute | solution.py:29
  132.2 7.5 %collective-permute-start.21 = (bf16[64,512]{1,0:T(8,128)(2,1)S(1)}, bf16[64,512]{1,0:T(8,128)(2,1)S(1)}, u32[]{:S(2)}, u32[]{:S(2)}) collective-permute-start(bf16[64,512]{1,0:T(8,128)(2,1)S(1)} %fusion.9), channel_id=1, source_target_pairs={{0,18},{1,19},{2,16},{3,17},{4,22},{5,23},{6,20},{7,21},{8,26},{9,... | collective-permute-start | bytes 196616 | tf_op jit(solution)/shard_map/ppermute | solution.py:29
  136.9 5.2 %collective-permute-start.22 = (bf16[64,512]{1,0:T(8,128)(2,1)S(1)}, bf16[64,512]{1,0:T(8,128)(2,1)S(1)}, u32[]{:S(2)}, u32[]{:S(2)}) collective-permute-start(bf16[64,512]{1,0:T(8,128)(2,1)S(1)} %fusion.9), channel_id=1, source_target_pairs={{0,26},{1,27},{2,24},{3,25},{4,30},{5,31},{6,28},{7,29},{8,2},{9,3... | collective-permute-start | bytes 196616 | tf_op jit(solution)/shard_map/ppermute | solution.py:29
  145.3 6.2 %collective-permute-start.23 = (bf16[64,512]{1,0:T(8,128)(2,1)S(1)}, bf16[64,512]{1,0:T(8,128)(2,1)S(1)}, u32[]{:S(2)}, u32[]{:S(2)}) collective-permute-start(bf16[64,512]{1,0:T(8,128)(2,1)S(1)} %get-tuple-element.17), channel_id=1, source_target_pairs={{0,8},{1,9},{2,10},{3,11},{4,12},{5,13},{6,14},{7,15},{8,16},{9,17... | collective-permute-start | bytes 196616 | tf_op jit(solution)/shard_map/ppermute | solution.py:29
  146.2 6.7 %collective-permute-start.24 = (bf16[64,512]{1,0:T(8,128)(2,1)S(1)}, bf16[64,512]{1,0:T(8,128)(2,1)S(1)}, u32[]{:S(2)}, u32[]{:S(2)}) collective-permute-start(bf16[64,512]{1,0:T(8,128)(2,1)S(1)} %get-tuple-element.17), channel_id=1, source_target_pairs={{0,16},{1,17},{2,18},{3,19},{4,20},{5,21},{6,22},{7,23},{8,24},{9,... | collective-permute-start | bytes 196616 | tf_op jit(solution)/shard_map/ppermute | solution.py:29
  148.9 4.7 %collective-permute-start.25 = (bf16[64,512]{1,0:T(8,128)(2,1)S(1)}, bf16[64,512]{1,0:T(8,128)(2,1)S(1)}, u32[]{:S(2)}, u32[]{:S(2)}) collective-permute-start(bf16[64,512]{1,0:T(8,128)(2,1)S(1)} %get-tuple-element.17), channel_id=1, source_target_pairs={{0,24},{1,25},{2,26},{3,27},{4,28},{5,29},{6,30},{7,31},{8,0},{9,1... | collective-permute-start | bytes 196616 | tf_op jit(solution)/shard_map/ppermute | solution.py:29
  154.5 7.6 %collective-permute-start.26 = (bf16[64,512]{1,0:T(8,128)(2,1)S(1)}, bf16[64,512]{1,0:T(8,128)(2,1)S(1)}, u32[]{:S(2)}, u32[]{:S(2)}) collective-permute-start(bf16[64,512]{1,0:T(8,128)(2,1)S(1)} %get-tuple-element.15), channel_id=1, source_target_pairs={{0,8},{1,9},{2,10},{3,11},{4,12},{5,13},{6,14},{7,15},{8,16},{9,17... | collective-permute-start | bytes 196616 | tf_op jit(solution)/shard_map/ppermute | solution.py:29
  158.8 5.9 %collective-permute-start.27 = (bf16[64,512]{1,0:T(8,128)(2,1)S(1)}, bf16[64,512]{1,0:T(8,128)(2,1)S(1)}, u32[]{:S(2)}, u32[]{:S(2)}) collective-permute-start(bf16[64,512]{1,0:T(8,128)(2,1)S(1)} %get-tuple-element.15), channel_id=1, source_target_pairs={{0,16},{1,17},{2,18},{3,19},{4,20},{5,21},{6,22},{7,23},{8,24},{9,... | collective-permute-start | bytes 196616 | tf_op jit(solution)/shard_map/ppermute | solution.py:29
  161.2 4.3 %collective-permute-start.28 = (bf16[64,512]{1,0:T(8,128)(2,1)S(1)}, bf16[64,512]{1,0:T(8,128)(2,1)S(1)}, u32[]{:S(2)}, u32[]{:S(2)}) collective-permute-start(bf16[64,512]{1,0:T(8,128)(2,1)S(1)} %get-tuple-element.15), channel_id=1, source_target_pairs={{0,24},{1,25},{2,26},{3,27},{4,28},{5,29},{6,30},{7,31},{8,0},{9,1... | collective-permute-start | bytes 196616 | tf_op jit(solution)/shard_map/ppermute | solution.py:29
  166.4 6.1 %collective-permute-start.31 = (bf16[64,512]{1,0:T(8,128)(2,1)S(1)}, bf16[64,512]{1,0:T(8,128)(2,1)S(1)}, u32[]{:S(2)}, u32[]{:S(2)}) collective-permute-start(bf16[64,512]{1,0:T(8,128)(2,1)S(1)} %get-tuple-element.13), channel_id=1, source_target_pairs={{0,8},{1,9},{2,10},{3,11},{4,12},{5,13},{6,14},{7,15},{8,16},{9,17... | collective-permute-start | bytes 196616 | tf_op jit(solution)/shard_map/ppermute | solution.py:29
  167.9 6.1 %collective-permute-start.32 = (bf16[64,512]{1,0:T(8,128)(2,1)S(1)}, bf16[64,512]{1,0:T(8,128)(2,1)S(1)}, u32[]{:S(2)}, u32[]{:S(2)}) collective-permute-start(bf16[64,512]{1,0:T(8,128)(2,1)S(1)} %get-tuple-element.13), channel_id=1, source_target_pairs={{0,16},{1,17},{2,18},{3,19},{4,20},{5,21},{6,22},{7,23},{8,24},{9,... | collective-permute-start | bytes 196616 | tf_op jit(solution)/shard_map/ppermute | solution.py:29
  170.8 4.3 %collective-permute-start.33 = (bf16[64,512]{1,0:T(8,128)(2,1)S(1)}, bf16[64,512]{1,0:T(8,128)(2,1)S(1)}, u32[]{:S(2)}, u32[]{:S(2)}) collective-permute-start(bf16[64,512]{1,0:T(8,128)(2,1)S(1)} %get-tuple-element.13), channel_id=1, source_target_pairs={{0,24},{1,25},{2,26},{3,27},{4,28},{5,29},{6,30},{7,31},{8,0},{9,1... | collective-permute-start | bytes 196616 | tf_op jit(solution)/shard_map/ppermute | solution.py:29
  176.0 5.3 %collective-permute-start.36 = (f32[64,256]{1,0:T(8,128)S(1)}, f32[64,256]{1,0:T(8,128)S(1)}, u32[]{:S(2)}, u32[]{:S(2)}) collective-permute-start(f32[64,256]{1,0:T(8,128)S(1)} %get-tuple-element.9), channel_id=1, source_target_pairs={{0,1},{1,0},{2,3},{3,2},{4,5},{5,4},{6,7},{7,6},{8,9},{9,8},{10,11... | collective-permute-start | bytes 196616 | tf_op jit(solution)/shard_map/ppermute | solution.py:29
  176.1 4.0 %collective-permute-start.37 = (bf16[64,256]{1,0:T(8,128)(2,1)S(1)}, bf16[64,256]{1,0:T(8,128)(2,1)S(1)}, u32[]{:S(2)}, u32[]{:S(2)}) collective-permute-start(bf16[64,256]{1,0:T(8,128)(2,1)S(1)} %get-tuple-element.33), channel_id=1, source_target_pairs={{0,4},{1,5},{2,6},{3,7},{4,0},{5,1},{6,2},{7,3},{8,12},{9,13},{10,... | collective-permute-start | bytes 98312 | tf_op jit(solution)/shard_map/ppermute | solution.py:29
  178.0 3.3 %collective-permute-start.38 = (bf16[64,256]{1,0:T(8,128)(2,1)S(1)}, bf16[64,256]{1,0:T(8,128)(2,1)S(1)}, u32[]{:S(2)}, u32[]{:S(2)}) collective-permute-start(bf16[64,256]{1,0:T(8,128)(2,1)S(1)} %get-tuple-element.32), channel_id=1, source_target_pairs={{0,5},{1,4},{2,7},{3,6},{4,1},{5,0},{6,3},{7,2},{8,13},{9,12},{10,... | collective-permute-start | bytes 98312 | tf_op jit(solution)/shard_map/ppermute | solution.py:29
where the time goes:
time: 183 us; the launch traced here: 182 us
  starting transfers between devices  90.2 us (49%)
  waiting for transfers between devices  60.2 us (33%)
  Pallas kernels  13.6 us (7%)
  other arithmetic  6.34 us (3%)
  matrix products  6.25 us (3%)
  local copies, waits for them, and re-layouts  5.21 us (3%)
    ppermute x39, starting transfers between devices, send(): return lax.ppermute(value, AXES, pairs)  82.8 us
    ppermute x39, waiting for transfers between devices, send(): return lax.ppermute(value, AXES, pairs)  47.8 us
    all_to_all x1, waiting for transfers between devices, local(): came = lax.all_to_all(parts, ('cz', 'cy', 'rc'), 0, 0)  12.4 us
    pallas_call x1, Pallas kernels, prior_parts(): pl.pallas_call(kernel, grid_spec=pltpu.PrefetchScalarGridSpec(num_scalar_...  8.01 us
    all_to_all x1, starting transfers between devices, local(): came = lax.all_to_all(parts, ('cz', 'cy', 'rc'), 0, 0)  7.42 us
    dot_general x14, matrix products, apply(): lax.dot_general(vector, piece, (((1,), (1,)), ((), ())), preferred_elemen...  6.25 us
    pallas_call x2, Pallas kernels, picked(): pl.pallas_call(kernel, in_specs=[pl.BlockSpec(memory_space=pltpu.SMEM)] +...  5.64 us
    select_n x8, other arithmetic, pick(): return lax.optimization_barrier(jnp.where(core == 0, even, odd))  5.15 us
  transfers between devices with their start and end apart: 40, of which 23 were waited for; matrix products, arithmetic and copies ran while one was open for 7% of the time, Pallas kernels for 3%

commit v1 on v0

--- a/solution.py
+++ b/solution.py
@@ -96,15 +96,16 @@
             compiler_params=pltpu.CompilerParams(vmem_limit_bytes=(4 + 4 * count) * 1024 * 1024),
         )(jnp.stack([flag, why]).astype(jnp.int32), *vectors, own, own_y, other, other_y)
 
-    def prior_parts(zed, why, right_side, prior_solution, factor_codes, block_scale):
+    def prior_parts(right_side, prior_solution, factor_codes, block_scale):
         each, width = right_side.shape
         panel, depth = factor_codes.shape
         blocks = block_scale.shape[1]
         deep = depth // blocks
         chunk = 2 * each
 
-        def kernel(place_ref, scale_ref, right_ref, prior_ref, codes_ref, out_ref, scaled, total):
+        def kernel(scale_ref, right_ref, prior_ref, codes_ref, out_ref, scaled, total):
             step = pl.program_id(0)
+            zed, why = lax.axis_index("cz"), lax.axis_index("cy")
 
             @pl.when(step == 0)
             def _():
@@ -116,9 +117,9 @@
                 codes_ref[...], scaled[...], preferred_element_type=jnp.float32
             )
 
-            @pl.when(step == place_ref[0])
-            def _():
-                rows = pl.ds(pl.multiple_of(place_ref[1] * each, each), each)
+            @pl.when(step == zed)
+            def _():
+                rows = pl.ds(pl.multiple_of(why * each, each), each)
                 total[rows, :] += right_ref[...]
 
             out_ref[0] = total[...].T.astype(bf16)
@@ -126,15 +127,15 @@
         return pl.pallas_call(
             kernel,
             grid_spec=pltpu.PrefetchScalarGridSpec(
-                num_scalar_prefetch=1,
+                num_scalar_prefetch=0,
                 grid=(panel // chunk,),
                 in_specs=[
                     pl.BlockSpec(memory_space=pltpu.SMEM),
-                    pl.BlockSpec((each, width), lambda i, p: (0, 0)),
-                    pl.BlockSpec((depth, width), lambda i, p: (0, 0)),
-                    pl.BlockSpec((chunk, depth), lambda i, p: (i, 0)),
+                    pl.BlockSpec((each, width), lambda i: (0, 0)),
+                    pl.BlockSpec((depth, width), lambda i: (0, 0)),
+                    pl.BlockSpec((chunk, depth), lambda i: (i, 0)),
                 ],
-                out_specs=pl.BlockSpec((1, width, chunk), lambda i, p: (i, 0, 0)),
+                out_specs=pl.BlockSpec((1, width, chunk), lambda i: (i, 0, 0)),
                 scratch_shapes=[
                     pltpu.VMEM((depth, width), bf16),
                     pltpu.VMEM((chunk, width), jnp.float32),
@@ -147,7 +148,7 @@
                 transcendentals=0,
             ),
             compiler_params=pltpu.CompilerParams(vmem_limit_bytes=60 * 1024 * 1024),
-        )(jnp.stack([zed, why]).astype(jnp.int32), block_scale, right_side, prior_solution, factor_codes)
+        )(block_scale, right_side, prior_solution, factor_codes)
 
     def local(right_side, prior_solution, factor_codes, block_scale, diag_inverse, inner_factor):
         each, width = right_side.shape
@@ -228,7 +229,7 @@
             inv_odd[turn] = (near_odd, pick(inverse_yc[turn], inverse_y[turn]))
             link[turn] = (near_link, pick(pair_yc[turn], pair_y[turn]))
 
-        parts = prior_parts(zed, why, right_side, prior_solution, factor_codes, block_scale)
+        parts = prior_parts(right_side, prior_solution, factor_codes, block_scale)
         parts = parts.reshape(count_z * 4, part, chunk)
         came = lax.all_to_all(parts, ("cz", "cy", "rc"), 0, 0)
         came = came.reshape(count_z * 2, 2, part, chunk)

time: 183 us -> 182 us (level)
  no operation moved by 1% of the time
where the time goes in v1:
time: 182 us; the launch traced here: 181 us
  starting transfers between devices  90.1 us (50%)
  waiting for transfers between devices  60.2 us (33%)
  Pallas kernels  13 us (7%)
  matrix products  6.26 us (3%)
  other arithmetic  5.76 us (3%)
  local copies, waits for them, and re-layouts  5.21 us (3%)
    ppermute x39, starting transfers between devices, send(): return lax.ppermute(value, AXES, pairs)  82.7 us
    ppermute x39, waiting for transfers between devices, send(): return lax.ppermute(value, AXES, pairs)  47.8 us
    all_to_all x1, waiting for transfers between devices, local(): came = lax.all_to_all(parts, ('cz', 'cy', 'rc'), 0, 0)  12.4 us
    all_to_all x1, starting transfers between devices, local(): came = lax.all_to_all(parts, ('cz', 'cy', 'rc'), 0, 0)  7.41 us
    pallas_call x1, Pallas kernels, prior_parts(): pl.pallas_call(kernel, grid_spec=pltpu.PrefetchScalarGridSpec(num_scalar_...  7.35 us
    dot_general x14, matrix products, apply(): lax.dot_general(vector, piece, (((1,), (1,)), ((), ())), preferred_elemen...  6.26 us
    pallas_call x2, Pallas kernels, picked(): pl.pallas_call(kernel, in_specs=[pl.BlockSpec(memory_space=pltpu.SMEM)] +...  5.64 us
    select_n x8, other arithmetic, pick(): return lax.optimization_barrier(jnp.where(core == 0, even, odd))  5.15 us
  transfers between devices with their start and end apart: 40, of which 23 were waited for; matrix products, arithmetic and copies ran while one was open for 7% of the time, Pallas kernels for 3%

profile of v1, /device:TPU:0, one launch (start us, length us, event | category | flops | bytes accessed | tf_op | source)
XLA Modules:
  0.0 181.0 jit_solution(13713452574014576829)
XLA Ops:
  0.0 7.4 %shard_map.64 = bf16[4,256,512]{2,1,0:T(8,128)(2,1)} custom-call(f32[1,8]{1,0:T(1,128)} %scale_ref.1, f32[256,256]{1,0:T(8,128)} %right_ref.1, bf16[2048,256]{1,0:T(8,128)(2,1)} %prior_ref.1, bf16[2048,2048]{1,0:T(8,128)(2,1)} %codes_ref.1), custom_call_target="tpu_custom_call" | custom-call | flops 2147483648 | bytes 10485760 | tf_op jit(solution)/shard_map/pallas_call | solution.py:127
  7.4 7.4 %all-to-all-start = ((bf16[16,64,512]{2,1,0:T(8,128)(2,1)}), bf16[16,64,512]{2,1,0:T(8,128)(2,1)S(1)}, u32[]{:S(2)}, u32[]{:S(2)}) async-start(bf16[16,64,512]{2,1,0:T(8,128)(2,1)} %bitcast.54), calls=%async_computation | async-start | bytes 2097152 | tf_op jit(solution)/shard_map/all_to_all | solution.py:234
  14.8 3.8 %collective-permute-start.4 = (bf16[256,2048]{1,0:T(8,128)(2,1)}, bf16[256,2048]{1,0:T(8,128)(2,1)}, u32[]{:S(2)}, u32[]{:S(2)}) collective-permute-start(bf16[256,2048]{1,0:T(8,128)(2,1)} %bitcast.4), channel_id=1, source_target_pairs={{0,4},{1,5},{2,6},{4,0},{5,1},{6,2},{8,12},{9,13},{10,14},{12,8},{... | collective-permute-start | bytes 3145736 | tf_op jit(solution)/shard_map/ppermute | solution.py:29
  18.7 2.3 %dynamic-slice_bitcast_fusion = bf16[256,2048]{1,0:T(8,128)(2,1)} fusion(bf16[1,4,256,2048]{3,2,1,0:T(8,128)(2,1)} %param.11, s32[]{:T(128)S(6)} %select_n.265), kind=kLoop, calls=%fused_computation.5 | loop fusion | bytes 2097156 | tf_op jit(solution)/shard_map/jit(dynamic_index_in_dim)/squeeze | solution.py:213
  21.0 1.6 collective-permute-start.14
  22.6 0.8 collective-permute-start.13
  23.5 1.7 slice_bitcast_fusion.refs_1_.refs_2_
  25.3 12.4 %all-to-all-done = bf16[16,64,512]{2,1,0:T(8,128)(2,1)S(1)} async-done(((bf16[16,64,512]{2,1,0:T(8,128)(2,1)}), bf16[16,64,512]{2,1,0:T(8,128)(2,1)S(1)}, u32[]{:S(2)}, u32[]{:S(2)}) %all-to-all-start) | async-done | bytes 1048608 | tf_op jit(solution)/shard_map/all_to_all | solution.py:234
  37.8 3.3 %collective-permute-start = (bf16[64,512]{1,0:T(8,128)(2,1)S(1)}, bf16[64,512]{1,0:T(8,128)(2,1)S(1)}, u32[]{:S(2)}, u32[]{:S(2)}) collective-permute-start(bf16[64,512]{1,0:T(8,128)(2,1)S(1)} %get-tuple-element.23), channel_id=1, source_target_pairs={{0,8},{1,9},{2,10},{3,11},{4,12},{5,13},{6,14},{7,15},{8,16},{9,17... | collective-permute-start | bytes 196616 | tf_op jit(solution)/shard_map/ppermute | solution.py:29
  41.1 11.1 %collective-permute-done.4 = bf16[256,2048]{1,0:T(8,128)(2,1)} collective-permute-done((bf16[256,2048]{1,0:T(8,128)(2,1)}, bf16[256,2048]{1,0:T(8,128)(2,1)}, u32[]{:S(2)}, u32[]{:S(2)}) %collective-permute-start.4) | collective-permute-done | bytes 1048608 | tf_op jit(solution)/shard_map/ppermute | solution.py:29
  52.3 0.7 collective-permute-start.29
  53.0 0.7 collective-permute-start.34
  53.8 2.4 %collective-permute-start.1 = (bf16[64,512]{1,0:T(8,128)(2,1)S(1)}, bf16[64,512]{1,0:T(8,128)(2,1)S(1)}, u32[]{:S(2)}, u32[]{:S(2)}) collective-permute-start(bf16[64,512]{1,0:T(8,128)(2,1)S(1)} %get-tuple-element.23), channel_id=1, source_target_pairs={{0,16},{1,17},{2,18},{3,19},{4,20},{5,21},{6,22},{7,23},{8,24},{9,... | collective-permute-start | bytes 196616 | tf_op jit(solution)/shard_map/ppermute | solution.py:29
  56.3 1.7 broadcast_select_fusion.3
  57.9 2.7 %collective-permute-done.1 = bf16[64,512]{1,0:T(8,128)(2,1)S(1)} collective-permute-done((bf16[64,512]{1,0:T(8,128)(2,1)S(1)}, bf16[64,512]{1,0:T(8,128)(2,1)S(1)}, u32[]{:S(2)}, u32[]{:S(2)}) %collective-permute-start.1) | collective-permute-done | bytes 65568 | tf_op jit(solution)/shard_map/ppermute | solution.py:29
  60.6 3.3 %collective-permute-start.2 = (bf16[64,512]{1,0:T(8,128)(2,1)S(1)}, bf16[64,512]{1,0:T(8,128)(2,1)S(1)}, u32[]{:S(2)}, u32[]{:S(2)}) collective-permute-start(bf16[64,512]{1,0:T(8,128)(2,1)S(1)} %get-tuple-element.23), channel_id=1, source_target_pairs={{0,24},{1,25},{2,26},{3,27},{4,28},{5,29},{6,30},{7,31},{8,0},{9,1... | collective-permute-start | bytes 196616 | tf_op jit(solution)/shard_map/ppermute | solution.py:29
  63.9 1.4 broadcast_select_fusion.5
  65.2 0.5 collective-permute-done.2
  65.9 0.8 collective-permute-start.10
  66.7 0.6 collective-permute-start.15
  67.8 1.5 broadcast_select_fusion.2
  69.8 0.5 broadcast_select_fusion.25
  70.3 1.2 collective-permute-done.15
  71.6 4.8 %collective-permute-start.7 = (bf16[64,512]{1,0:T(8,128)(2,1)S(1)}, bf16[64,512]{1,0:T(8,128)(2,1)S(1)}, u32[]{:S(2)}, u32[]{:S(2)}) collective-permute-start(bf16[64,512]{1,0:T(8,128)(2,1)S(1)} %get-tuple-element.21), channel_id=1, source_target_pairs={{0,16},{1,17},{2,18},{3,19},{4,20},{5,21},{6,22},{7,23},{8,24},{9,... | collective-permute-start | bytes 196616 | tf_op jit(solution)/shard_map/ppermute | solution.py:29
  76.6 1.4 collective-permute-done.6
  78.0 2.8 %collective-permute-done.7 = bf16[64,512]{1,0:T(8,128)(2,1)S(1)} collective-permute-done((bf16[64,512]{1,0:T(8,128)(2,1)S(1)}, bf16[64,512]{1,0:T(8,128)(2,1)S(1)}, u32[]{:S(2)}, u32[]{:S(2)}) %collective-permute-start.7) | collective-permute-done | bytes 65568 | tf_op jit(solution)/shard_map/ppermute | solution.py:29
  80.9 1.3 collective-permute-done.8
  82.7 0.5 broadcast_select_fusion.23
  83.2 0.6 collective-permute-start.16
  83.9 2.3 %collective-permute-start.17 = (bf16[64,512]{1,0:T(8,128)(2,1)S(1)}, bf16[64,512]{1,0:T(8,128)(2,1)S(1)}, u32[]{:S(2)}, u32[]{:S(2)}) collective-permute-start(bf16[64,512]{1,0:T(8,128)(2,1)S(1)} %get-tuple-element.19), channel_id=1, source_target_pairs={{0,16},{1,17},{2,18},{3,19},{4,20},{5,21},{6,22},{7,23},{8,24},{9,... | collective-permute-start | bytes 196616 | tf_op jit(solution)/shard_map/ppermute | solution.py:29
  86.2 1.1 collective-permute-start.18
  87.3 2.7 %collective-permute-done.16 = bf16[64,512]{1,0:T(8,128)(2,1)S(1)} collective-permute-done((bf16[64,512]{1,0:T(8,128)(2,1)S(1)}, bf16[64,512]{1,0:T(8,128)(2,1)S(1)}, u32[]{:S(2)}, u32[]{:S(2)}) %collective-permute-start.16) | collective-permute-done | bytes 65568 | tf_op jit(solution)/shard_map/ppermute | solution.py:29
  90.1 2.0 %collective-permute-done.17 = bf16[64,512]{1,0:T(8,128)(2,1)S(1)} collective-permute-done((bf16[64,512]{1,0:T(8,128)(2,1)S(1)}, bf16[64,512]{1,0:T(8,128)(2,1)S(1)}, u32[]{:S(2)}, u32[]{:S(2)}) %collective-permute-start.17) | collective-permute-done | bytes 65568 | tf_op jit(solution)/shard_map/ppermute | solution.py:29
  93.0 35.3 %collective-permute-start.19 = (bf16[64,512]{1,0:T(8,128)(2,1)S(1)}, bf16[64,512]{1,0:T(8,128)(2,1)S(1)}, u32[]{:S(2)}, u32[]{:S(2)}) collective-permute-start(bf16[64,512]{1,0:T(8,128)(2,1)S(1)} %fusion.9), channel_id=1, source_target_pairs={{0,2},{1,3},{2,0},{3,1},{4,6},{5,7},{6,4},{7,5},{8,10},{9,11},{10,... | collective-permute-start | bytes 196616 | tf_op jit(solution)/shard_map/ppermute | solution.py:29
  128.4 2.6 %collective-permute-start.20 = (bf16[64,512]{1,0:T(8,128)(2,1)S(1)}, bf16[64,512]{1,0:T(8,128)(2,1)S(1)}, u32[]{:S(2)}, u32[]{:S(2)}) collective-permute-start(bf16[64,512]{1,0:T(8,128)(2,1)S(1)} %fusion.9), channel_id=1, source_target_pairs={{0,10},{1,11},{2,8},{3,9},{4,14},{5,15},{6,12},{7,13},{8,18},{9,19... | collective-permute-start | bytes 196616 | tf_op jit(solution)/shard_map/ppermute | solution.py:29
  131.0 1.8 %collective-permute-start.21 = (bf16[64,512]{1,0:T(8,128)(2,1)S(1)}, bf16[64,512]{1,0:T(8,128)(2,1)S(1)}, u32[]{:S(2)}, u32[]{:S(2)}) collective-permute-start(bf16[64,512]{1,0:T(8,128)(2,1)S(1)} %fusion.9), channel_id=1, source_target_pairs={{0,18},{1,19},{2,16},{3,17},{4,22},{5,23},{6,20},{7,21},{8,26},{9,... | collective-permute-start | bytes 196616 | tf_op jit(solution)/shard_map/ppermute | solution.py:29
  132.8 2.9 %collective-permute-done.20 = bf16[64,512]{1,0:T(8,128)(2,1)S(1)} collective-permute-done((bf16[64,512]{1,0:T(8,128)(2,1)S(1)}, bf16[64,512]{1,0:T(8,128)(2,1)S(1)}, u32[]{:S(2)}, u32[]{:S(2)}) %collective-permute-start.20) | collective-permute-done | bytes 65568 | tf_op jit(solution)/shard_map/ppermute | solution.py:29
  135.7 0.9 collective-permute-start.22
  136.6 1.8 collective-permute-done.21
  138.4 2.4 %collective-permute-done.22 = bf16[64,512]{1,0:T(8,128)(2,1)S(1)} collective-permute-done((bf16[64,512]{1,0:T(8,128)(2,1)S(1)}, bf16[64,512]{1,0:T(8,128)(2,1)S(1)}, u32[]{:S(2)}, u32[]{:S(2)}) %collective-permute-start.22) | collective-permute-done | bytes 65568 | tf_op jit(solution)/shard_map/ppermute | solution.py:29
  141.0 2.1 %shard_map.65 = f32[64,512]{1,0:T(8,128)S(1)} custom-call(s32[2]{0:T(128)S(1)} %pad_add_fusion.flags, bf16[64,2048]{1,0:T(8,128)(2,1)S(1)} %collective-permute-done.9.refs_0_, bf16[2,256,2048]{2,1,0:T(8,128)(2,1)S(1)} %slice_bitcast_fusion.refs_1_.refs_2_, bf16[2,256,2048]{2,1,0:T(8,128)(2,1)S(1)} %collective-permute-done.10.refs_2_.refs_3_, ...), custom_call_target="tpu_custom_call" | custom-call | flops 134217728 | bytes 2097152 | tf_op jit(solution)/shard_map/pallas_call | solution.py:82
  144.1 0.8 collective-permute-start.23
  145.0 2.6 %collective-permute-start.24 = (bf16[64,512]{1,0:T(8,128)(2,1)S(1)}, bf16[64,512]{1,0:T(8,128)(2,1)S(1)}, u32[]{:S(2)}, u32[]{:S(2)}) collective-permute-start(bf16[64,512]{1,0:T(8,128)(2,1)S(1)} %get-tuple-element.17), channel_id=1, source_target_pairs={{0,16},{1,17},{2,18},{3,19},{4,20},{5,21},{6,22},{7,23},{8,24},{9,... | collective-permute-start | bytes 196616 | tf_op jit(solution)/shard_map/ppermute | solution.py:29
  147.6 0.6 collective-permute-start.25
  148.3 2.1 %collective-permute-done.23 = bf16[64,512]{1,0:T(8,128)(2,1)S(1)} collective-permute-done((bf16[64,512]{1,0:T(8,128)(2,1)S(1)}, bf16[64,512]{1,0:T(8,128)(2,1)S(1)}, u32[]{:S(2)}, u32[]{:S(2)}) %collective-permute-start.23) | collective-permute-done | bytes 65568 | tf_op jit(solution)/shard_map/ppermute | solution.py:29
  150.4 1.3 collective-permute-done.24
  151.7 0.6 collective-permute-done.25
  152.8 0.5 broadcast_select_fusion.17
  153.3 0.7 collective-permute-start.26
  154.1 3.5 %shard_map.66 = f32[64,512]{1,0:T(8,128)S(1)} custom-call(s32[2]{0:T(128)S(1)} %pad_add_fusion.1.flags, bf16[64,2048]{1,0:T(8,128)(2,1)S(1)} %collective-permute-done.9.refs_0_, bf16[64,2048]{1,0:T(8,128)(2,1)S(1)} %negate_select_fusion.refs_1_, bf16[2,256,2048]{2,1,0:T(8,128)(2,1)S(1)} %slice_bitcast_fusion.refs_1_.refs_2_, ...), custom_call_target="tpu_custom_call" | custom-call | flops 268435456 | bytes 4194304 | tf_op jit(solution)/shard_map/pallas_call | solution.py:82
  157.6 2.4 %collective-permute-start.27 = (bf16[64,512]{1,0:T(8,128)(2,1)S(1)}, bf16[64,512]{1,0:T(8,128)(2,1)S(1)}, u32[]{:S(2)}, u32[]{:S(2)}) collective-permute-start(bf16[64,512]{1,0:T(8,128)(2,1)S(1)} %get-tuple-element.15), channel_id=1, source_target_pairs={{0,16},{1,17},{2,18},{3,19},{4,20},{5,21},{6,22},{7,23},{8,24},{9,... | collective-permute-start | bytes 196616 | tf_op jit(solution)/shard_map/ppermute | solution.py:29
  160.0 0.9 collective-permute-start.28
  160.9 2.6 %collective-permute-done.27 = bf16[64,512]{1,0:T(8,128)(2,1)S(1)} collective-permute-done((bf16[64,512]{1,0:T(8,128)(2,1)S(1)}, bf16[64,512]{1,0:T(8,128)(2,1)S(1)}, u32[]{:S(2)}, u32[]{:S(2)}) %collective-permute-start.27) | collective-permute-done | bytes 65568 | tf_op jit(solution)/shard_map/ppermute | solution.py:29
  163.5 0.7 collective-permute-done.28
  164.7 0.5 broadcast_select_fusion.15
  165.2 1.4 collective-permute-start.31
  166.7 2.9 %collective-permute-start.32 = (bf16[64,512]{1,0:T(8,128)(2,1)S(1)}, bf16[64,512]{1,0:T(8,128)(2,1)S(1)}, u32[]{:S(2)}, u32[]{:S(2)}) collective-permute-start(bf16[64,512]{1,0:T(8,128)(2,1)S(1)} %get-tuple-element.13), channel_id=1, source_target_pairs={{0,16},{1,17},{2,18},{3,19},{4,20},{5,21},{6,22},{7,23},{8,24},{9,... | collective-permute-start | bytes 196616 | tf_op jit(solution)/shard_map/ppermute | solution.py:29
  169.6 1.8 collective-permute-done.31
  171.4 1.4 collective-permute-done.32
  172.8 1.1 collective-permute-done.33
  174.9 1.9 %collective-permute-start.37 = (bf16[64,256]{1,0:T(8,128)(2,1)S(1)}, bf16[64,256]{1,0:T(8,128)(2,1)S(1)}, u32[]{:S(2)}, u32[]{:S(2)}) collective-permute-start(bf16[64,256]{1,0:T(8,128)(2,1)S(1)} %get-tuple-element.33), channel_id=1, source_target_pairs={{0,4},{1,5},{2,6},{3,7},{4,0},{5,1},{6,2},{7,3},{8,12},{9,13},{10,... | collective-permute-start | bytes 98312 | tf_op jit(solution)/shard_map/ppermute | solution.py:29
  177.0 1.9 %collective-permute-done.37 = bf16[64,256]{1,0:T(8,128)(2,1)S(1)} collective-permute-done((bf16[64,256]{1,0:T(8,128)(2,1)S(1)}, bf16[64,256]{1,0:T(8,128)(2,1)S(1)}, u32[]{:S(2)}, u32[]{:S(2)}) %collective-permute-start.37) | collective-permute-done | bytes 32800 | tf_op jit(solution)/shard_map/ppermute | solution.py:29
  178.9 1.3 collective-permute-done.38
  180.2 0.8 copy.7
  (94 shorter events, 7.1 us)
Async XLA Ops:
  7.4 30.3 %all-to-all-start = ((bf16[16,64,512]{2,1,0:T(8,128)(2,1)}), bf16[16,64,512]{2,1,0:T(8,128)(2,1)S(1)}, u32[]{:S(2)}, u32[]{:S(2)}) async-start(bf16[16,64,512]{2,1,0:T(8,128)(2,1)} %bitcast.54), calls=%async_computation | async-start | bytes 2097152 | tf_op jit(solution)/shard_map/all_to_all | solution.py:234
  14.8 37.5 %collective-permute-start.4 = (bf16[256,2048]{1,0:T(8,128)(2,1)}, bf16[256,2048]{1,0:T(8,128)(2,1)}, u32[]{:S(2)}, u32[]{:S(2)}) collective-permute-start(bf16[256,2048]{1,0:T(8,128)(2,1)} %bitcast.4), channel_id=1, source_target_pairs={{0,4},{1,5},{2,6},{4,0},{5,1},{6,2},{8,12},{9,13},{10,14},{12,8},{... | collective-permute-start | bytes 3145736 | tf_op jit(solution)/shard_map/ppermute | solution.py:29
  18.6 34.4 %collective-permute-start.3 = (bf16[256,2048]{1,0:T(8,128)(2,1)}, bf16[256,2048]{1,0:T(8,128)(2,1)}, u32[]{:S(2)}, u32[]{:S(2)}) collective-permute-start(bf16[256,2048]{1,0:T(8,128)(2,1)} %bitcast.4), channel_id=1, source_target_pairs={{0,1},{1,0},{2,3},{3,2},{4,5},{5,4},{6,7},{7,6},{8,9},{9,8},{10,11... | collective-permute-start | bytes 3145736 | tf_op jit(solution)/shard_map/ppermute | solution.py:29
  21.0 44.9 %collective-permute-start.14 = (bf16[256,2048]{1,0:T(8,128)(2,1)}, bf16[256,2048]{1,0:T(8,128)(2,1)}, u32[]{:S(2)}, u32[]{:S(2)}) collective-permute-start(bf16[256,2048]{1,0:T(8,128)(2,1)} %dynamic-slice_bitcast_fusion), channel_id=1, source_target_pairs={{1,5},{5,1},{9,13},{13,9},{17,21},{21,17},{25,29},{29,25}} | collective-permute-start | bytes 3145736 | tf_op jit(solution)/shard_map/ppermute | solution.py:29
  22.6 31.1 %collective-permute-start.13 = (bf16[256,2048]{1,0:T(8,128)(2,1)}, bf16[256,2048]{1,0:T(8,128)(2,1)}, u32[]{:S(2)}, u32[]{:S(2)}) collective-permute-start(bf16[256,2048]{1,0:T(8,128)(2,1)} %dynamic-slice_bitcast_fusion), channel_id=1, source_target_pairs={{0,1},{1,0},{2,3},{3,2},{4,5},{5,4},{6,7},{7,6},{8,9},{9,8},{10,11... | collective-permute-start | bytes 3145736 | tf_op jit(solution)/shard_map/ppermute | solution.py:29
  37.8 16.0 %collective-permute-start = (bf16[64,512]{1,0:T(8,128)(2,1)S(1)}, bf16[64,512]{1,0:T(8,128)(2,1)S(1)}, u32[]{:S(2)}, u32[]{:S(2)}) collective-permute-start(bf16[64,512]{1,0:T(8,128)(2,1)S(1)} %get-tuple-element.23), channel_id=1, source_target_pairs={{0,8},{1,9},{2,10},{3,11},{4,12},{5,13},{6,14},{7,15},{8,16},{9,17... | collective-permute-start | bytes 196616 | tf_op jit(solution)/shard_map/ppermute | solution.py:29
  41.1 22.8 %copy-start = (bf16[1,4,256,2048]{3,2,1,0:T(8,128)(2,1)S(1)}, bf16[1,4,256,2048]{3,2,1,0:T(8,128)(2,1)}, u32[]{:S(2)}) copy-start(bf16[1,4,256,2048]{3,2,1,0:T(8,128)(2,1)} %param.11) | copy-start | bytes 12582916
  52.3 14.5 %collective-permute-start.29 = (bf16[256,2048]{1,0:T(8,128)(2,1)}, bf16[256,2048]{1,0:T(8,128)(2,1)S(1)}, u32[]{:S(2)}, u32[]{:S(2)}) collective-permute-start(bf16[256,2048]{1,0:T(8,128)(2,1)} %dynamic-slice_bitcast_fusion), channel_id=1, source_target_pairs={{3,7},{7,3},{11,15},{15,11},{19,23},{23,19},{27,31},{31,27}} | collective-permute-start | bytes 3145736 | tf_op jit(solution)/shard_map/ppermute | solution.py:29
  53.0 14.3 %collective-permute-start.34 = (bf16[256,2048]{1,0:T(8,128)(2,1)}, bf16[256,2048]{1,0:T(8,128)(2,1)S(1)}, u32[]{:S(2)}, u32[]{:S(2)}) collective-permute-start(bf16[256,2048]{1,0:T(8,128)(2,1)} %bitcast.4), channel_id=1, source_target_pairs={{3,7},{7,3},{11,15},{15,11},{19,23},{23,19},{27,31},{31,27}} | collective-permute-start | bytes 3145736 | tf_op jit(solution)/shard_map/ppermute | solution.py:29
  53.7 13.7 %collective-permute-start.5 = (bf16[256,2048]{1,0:T(8,128)(2,1)}, bf16[256,2048]{1,0:T(8,128)(2,1)S(1)}, u32[]{:S(2)}, u32[]{:S(2)}) collective-permute-start(bf16[256,2048]{1,0:T(8,128)(2,1)} %collective-permute-done.4), channel_id=1, source_target_pairs={{0,1},{1,0},{2,3},{3,2},{4,5},{5,4},{6,7},{7,6},{8,9},{9,8},{10,11... | collective-permute-start | bytes 3145736 | tf_op jit(solution)/shard_map/ppermute | solution.py:29
  53.8 6.8 %collective-permute-start.1 = (bf16[64,512]{1,0:T(8,128)(2,1)S(1)}, bf16[64,512]{1,0:T(8,128)(2,1)S(1)}, u32[]{:S(2)}, u32[]{:S(2)}) collective-permute-start(bf16[64,512]{1,0:T(8,128)(2,1)S(1)} %get-tuple-element.23), channel_id=1, source_target_pairs={{0,16},{1,17},{2,18},{3,19},{4,20},{5,21},{6,22},{7,23},{8,24},{9,... | collective-permute-start | bytes 196616 | tf_op jit(solution)/shard_map/ppermute | solution.py:29
  60.6 5.2 %collective-permute-start.2 = (bf16[64,512]{1,0:T(8,128)(2,1)S(1)}, bf16[64,512]{1,0:T(8,128)(2,1)S(1)}, u32[]{:S(2)}, u32[]{:S(2)}) collective-permute-start(bf16[64,512]{1,0:T(8,128)(2,1)S(1)} %get-tuple-element.23), channel_id=1, source_target_pairs={{0,24},{1,25},{2,26},{3,27},{4,28},{5,29},{6,30},{7,31},{8,0},{9,1... | collective-permute-start | bytes 196616 | tf_op jit(solution)/shard_map/ppermute | solution.py:29
  65.8 5.8 %collective-permute-start.11 = (bf16[2,256,2048]{2,1,0:T(8,128)(2,1)S(1)}, bf16[2,256,2048]{2,1,0:T(8,128)(2,1)S(1)}, u32[]{:S(2)}, u32[]{:S(2)}) collective-permute-start(bf16[2,256,2048]{2,1,0:T(8,128)(2,1)S(1)} %slice_bitcast_fusion.refs_1_.refs_2_), channel_id=1, source_target_pairs={{0,1},{1,0},{2,3},{3,2},{4,5},{5,4},{6,7},{7,6},{8,9},{9,8},{10,11... | collective-permute-start | bytes 6291464 | tf_op jit(solution)/shard_map/ppermute | solution.py:29
  65.9 10.6 %collective-permute-start.10 = (bf16[2,256,2048]{2,1,0:T(8,128)(2,1)S(1)}, bf16[2,256,2048]{2,1,0:T(8,128)(2,1)S(1)}, u32[]{:S(2)}, u32[]{:S(2)}) collective-permute-start(bf16[2,256,2048]{2,1,0:T(8,128)(2,1)S(1)} %slice_bitcast_fusion.refs_1_.refs_2_), channel_id=1, source_target_pairs={{2,6},{3,7},{6,2},{7,3},{10,14},{11,15},{14,10},{15,11},{18,22},{1... | collective-permute-start | bytes 6291464 | tf_op jit(solution)/shard_map/ppermute | solution.py:29
  66.7 4.7 %collective-permute-start.15 = (bf16[256,2048]{1,0:T(8,128)(2,1)}, bf16[256,2048]{1,0:T(8,128)(2,1)S(1)}, u32[]{:S(2)}, u32[]{:S(2)}) collective-permute-start(bf16[256,2048]{1,0:T(8,128)(2,1)} %collective-permute-done.14), channel_id=1, source_target_pairs={{0,1},{1,0},{2,3},{3,2},{4,5},{5,4},{6,7},{7,6},{8,9},{9,8},{10,11... | collective-permute-start | bytes 3145736 | tf_op jit(solution)/shard_map/ppermute | solution.py:29
  67.3 16.4 %collective-permute-start.30 = (bf16[256,2048]{1,0:T(8,128)(2,1)S(1)}, bf16[256,2048]{1,0:T(8,128)(2,1)S(1)}, u32[]{:S(2)}, u32[]{:S(2)}) collective-permute-start(bf16[256,2048]{1,0:T(8,128)(2,1)S(1)} %collective-permute-done.29), channel_id=1, source_target_pairs={{0,1},{1,0},{2,3},{3,2},{4,5},{5,4},{6,7},{7,6},{8,9},{9,8},{10,11... | collective-permute-start | bytes 3145736 | tf_op jit(solution)/shard_map/ppermute | solution.py:29
  67.4 77.5 %collective-permute-start.35 = (bf16[256,2048]{1,0:T(8,128)(2,1)S(1)}, bf16[256,2048]{1,0:T(8,128)(2,1)S(1)}, u32[]{:S(2)}, u32[]{:S(2)}) collective-permute-start(bf16[256,2048]{1,0:T(8,128)(2,1)S(1)} %collective-permute-done.34), channel_id=1, source_target_pairs={{0,1},{1,0},{2,3},{3,2},{4,5},{5,4},{6,7},{7,6},{8,9},{9,8},{10,11... | collective-permute-start | bytes 3145736 | tf_op jit(solution)/shard_map/ppermute | solution.py:29
  71.4 6.6 %collective-permute-start.6 = (bf16[64,512]{1,0:T(8,128)(2,1)S(1)}, bf16[64,512]{1,0:T(8,128)(2,1)S(1)}, u32[]{:S(2)}, u32[]{:S(2)}) collective-permute-start(bf16[64,512]{1,0:T(8,128)(2,1)S(1)} %get-tuple-element.21), channel_id=1, source_target_pairs={{0,8},{1,9},{2,10},{3,11},{4,12},{5,13},{6,14},{7,15},{8,16},{9,17... | collective-permute-start | bytes 196616 | tf_op jit(solution)/shard_map/ppermute | solution.py:29
  71.6 9.2 %collective-permute-start.7 = (bf16[64,512]{1,0:T(8,128)(2,1)S(1)}, bf16[64,512]{1,0:T(8,128)(2,1)S(1)}, u32[]{:S(2)}, u32[]{:S(2)}) collective-permute-start(bf16[64,512]{1,0:T(8,128)(2,1)S(1)} %get-tuple-element.21), channel_id=1, source_target_pairs={{0,16},{1,17},{2,18},{3,19},{4,20},{5,21},{6,22},{7,23},{8,24},{9,... | collective-permute-start | bytes 196616 | tf_op jit(solution)/shard_map/ppermute | solution.py:29
  76.5 5.7 %collective-permute-start.8 = (bf16[64,512]{1,0:T(8,128)(2,1)S(1)}, bf16[64,512]{1,0:T(8,128)(2,1)S(1)}, u32[]{:S(2)}, u32[]{:S(2)}) collective-permute-start(bf16[64,512]{1,0:T(8,128)(2,1)S(1)} %get-tuple-element.21), channel_id=1, source_target_pairs={{0,24},{1,25},{2,26},{3,27},{4,28},{5,29},{6,30},{7,31},{8,0},{9,1... | collective-permute-start | bytes 196616 | tf_op jit(solution)/shard_map/ppermute | solution.py:29
  78.0 62.9 %collective-permute-start.12 = (bf16[2,256,2048]{2,1,0:T(8,128)(2,1)S(1)}, bf16[2,256,2048]{2,1,0:T(8,128)(2,1)S(1)}, u32[]{:S(2)}, u32[]{:S(2)}) collective-permute-start(bf16[2,256,2048]{2,1,0:T(8,128)(2,1)S(1)} %collective-permute-done.10.refs_2_.refs_3_), channel_id=1, source_target_pairs={{0,1},{1,0},{2,3},{3,2},{4,5},{5,4},{6,7},{7,6},{8,9},{9,8},{10,11... | collective-permute-start | bytes 6291464 | tf_op jit(solution)/shard_map/ppermute | solution.py:29
  83.2 6.9 %collective-permute-start.16 = (bf16[64,512]{1,0:T(8,128)(2,1)S(1)}, bf16[64,512]{1,0:T(8,128)(2,1)S(1)}, u32[]{:S(2)}, u32[]{:S(2)}) collective-permute-start(bf16[64,512]{1,0:T(8,128)(2,1)S(1)} %get-tuple-element.19), channel_id=1, source_target_pairs={{0,8},{1,9},{2,10},{3,11},{4,12},{5,13},{6,14},{7,15},{8,16},{9,17... | collective-permute-start | bytes 196616 | tf_op jit(solution)/shard_map/ppermute | solution.py:29
  83.9 8.2 %collective-permute-start.17 = (bf16[64,512]{1,0:T(8,128)(2,1)S(1)}, bf16[64,512]{1,0:T(8,128)(2,1)S(1)}, u32[]{:S(2)}, u32[]{:S(2)}) collective-permute-start(bf16[64,512]{1,0:T(8,128)(2,1)S(1)} %get-tuple-element.19), channel_id=1, source_target_pairs={{0,16},{1,17},{2,18},{3,19},{4,20},{5,21},{6,22},{7,23},{8,24},{9,... | collective-permute-start | bytes 196616 | tf_op jit(solution)/shard_map/ppermute | solution.py:29
  86.2 5.8 %collective-permute-start.18 = (bf16[64,512]{1,0:T(8,128)(2,1)S(1)}, bf16[64,512]{1,0:T(8,128)(2,1)S(1)}, u32[]{:S(2)}, u32[]{:S(2)}) collective-permute-start(bf16[64,512]{1,0:T(8,128)(2,1)S(1)} %get-tuple-element.19), channel_id=1, source_target_pairs={{0,24},{1,25},{2,26},{3,27},{4,28},{5,29},{6,30},{7,31},{8,0},{9,1... | collective-permute-start | bytes 196616 | tf_op jit(solution)/shard_map/ppermute | solution.py:29
  93.0 38.0 %collective-permute-start.19 = (bf16[64,512]{1,0:T(8,128)(2,1)S(1)}, bf16[64,512]{1,0:T(8,128)(2,1)S(1)}, u32[]{:S(2)}, u32[]{:S(2)}) collective-permute-start(bf16[64,512]{1,0:T(8,128)(2,1)S(1)} %fusion.9), channel_id=1, source_target_pairs={{0,2},{1,3},{2,0},{3,1},{4,6},{5,7},{6,4},{7,5},{8,10},{9,11},{10,... | collective-permute-start | bytes 196616 | tf_op jit(solution)/shard_map/ppermute | solution.py:29
  128.3 12.8 %collective-permute-start.9 = (bf16[64,2048]{1,0:T(8,128)(2,1)S(1)}, bf16[64,2048]{1,0:T(8,128)(2,1)S(1)}, u32[]{:S(2)}, u32[]{:S(2)}) collective-permute-start(bf16[64,2048]{1,0:T(8,128)(2,1)S(1)} %negate_select_fusion.1), channel_id=1, source_target_pairs={{0,2},{1,3},{2,0},{3,1},{4,6},{5,7},{6,4},{7,5},{8,10},{9,11},{10,... | collective-permute-start | bytes 786440 | tf_op jit(solution)/shard_map/ppermute | solution.py:29
  128.4 7.3 %collective-permute-start.20 = (bf16[64,512]{1,0:T(8,128)(2,1)S(1)}, bf16[64,512]{1,0:T(8,128)(2,1)S(1)}, u32[]{:S(2)}, u32[]{:S(2)}) collective-permute-start(bf16[64,512]{1,0:T(8,128)(2,1)S(1)} %fusion.9), channel_id=1, source_target_pairs={{0,10},{1,11},{2,8},{3,9},{4,14},{5,15},{6,12},{7,13},{8,18},{9,19... | collective-permute-start | bytes 196616 | tf_op jit(solution)/shard_map/ppermute | solution.py:29
  131.0 7.5 %collective-permute-start.21 = (bf16[64,512]{1,0:T(8,128)(2,1)S(1)}, bf16[64,512]{1,0:T(8,128)(2,1)S(1)}, u32[]{:S(2)}, u32[]{:S(2)}) collective-permute-start(bf16[64,512]{1,0:T(8,128)(2,1)S(1)} %fusion.9), channel_id=1, source_target_pairs={{0,18},{1,19},{2,16},{3,17},{4,22},{5,23},{6,20},{7,21},{8,26},{9,... | collective-permute-start | bytes 196616 | tf_op jit(solution)/shard_map/ppermute | solution.py:29
  135.7 5.2 %collective-permute-start.22 = (bf16[64,512]{1,0:T(8,128)(2,1)S(1)}, bf16[64,512]{1,0:T(8,128)(2,1)S(1)}, u32[]{:S(2)}, u32[]{:S(2)}) collective-permute-start(bf16[64,512]{1,0:T(8,128)(2,1)S(1)} %fusion.9), channel_id=1, source_target_pairs={{0,26},{1,27},{2,24},{3,25},{4,30},{5,31},{6,28},{7,29},{8,2},{9,3... | collective-permute-start | bytes 196616 | tf_op jit(solution)/shard_map/ppermute | solution.py:29
  144.1 6.2 %collective-permute-start.23 = (bf16[64,512]{1,0:T(8,128)(2,1)S(1)}, bf16[64,512]{1,0:T(8,128)(2,1)S(1)}, u32[]{:S(2)}, u32[]{:S(2)}) collective-permute-start(bf16[64,512]{1,0:T(8,128)(2,1)S(1)} %get-tuple-element.17), channel_id=1, source_target_pairs={{0,8},{1,9},{2,10},{3,11},{4,12},{5,13},{6,14},{7,15},{8,16},{9,17... | collective-permute-start | bytes 196616 | tf_op jit(solution)/shard_map/ppermute | solution.py:29
  145.0 6.7 %collective-permute-start.24 = (bf16[64,512]{1,0:T(8,128)(2,1)S(1)}, bf16[64,512]{1,0:T(8,128)(2,1)S(1)}, u32[]{:S(2)}, u32[]{:S(2)}) collective-permute-start(bf16[64,512]{1,0:T(8,128)(2,1)S(1)} %get-tuple-element.17), channel_id=1, source_target_pairs={{0,16},{1,17},{2,18},{3,19},{4,20},{5,21},{6,22},{7,23},{8,24},{9,... | collective-permute-start | bytes 196616 | tf_op jit(solution)/shard_map/ppermute | solution.py:29
  147.6 4.7 %collective-permute-start.25 = (bf16[64,512]{1,0:T(8,128)(2,1)S(1)}, bf16[64,512]{1,0:T(8,128)(2,1)S(1)}, u32[]{:S(2)}, u32[]{:S(2)}) collective-permute-start(bf16[64,512]{1,0:T(8,128)(2,1)S(1)} %get-tuple-element.17), channel_id=1, source_target_pairs={{0,24},{1,25},{2,26},{3,27},{4,28},{5,29},{6,30},{7,31},{8,0},{9,1... | collective-permute-start | bytes 196616 | tf_op jit(solution)/shard_map/ppermute | solution.py:29
  153.3 7.6 %collective-permute-start.26 = (bf16[64,512]{1,0:T(8,128)(2,1)S(1)}, bf16[64,512]{1,0:T(8,128)(2,1)S(1)}, u32[]{:S(2)}, u32[]{:S(2)}) collective-permute-start(bf16[64,512]{1,0:T(8,128)(2,1)S(1)} %get-tuple-element.15), channel_id=1, source_target_pairs={{0,8},{1,9},{2,10},{3,11},{4,12},{5,13},{6,14},{7,15},{8,16},{9,17... | collective-permute-start | bytes 196616 | tf_op jit(solution)/shard_map/ppermute | solution.py:29
  157.6 5.9 %collective-permute-start.27 = (bf16[64,512]{1,0:T(8,128)(2,1)S(1)}, bf16[64,512]{1,0:T(8,128)(2,1)S(1)}, u32[]{:S(2)}, u32[]{:S(2)}) collective-permute-start(bf16[64,512]{1,0:T(8,128)(2,1)S(1)} %get-tuple-element.15), channel_id=1, source_target_pairs={{0,16},{1,17},{2,18},{3,19},{4,20},{5,21},{6,22},{7,23},{8,24},{9,... | collective-permute-start | bytes 196616 | tf_op jit(solution)/shard_map/ppermute | solution.py:29
  160.0 4.3 %collective-permute-start.28 = (bf16[64,512]{1,0:T(8,128)(2,1)S(1)}, bf16[64,512]{1,0:T(8,128)(2,1)S(1)}, u32[]{:S(2)}, u32[]{:S(2)}) collective-permute-start(bf16[64,512]{1,0:T(8,128)(2,1)S(1)} %get-tuple-element.15), channel_id=1, source_target_pairs={{0,24},{1,25},{2,26},{3,27},{4,28},{5,29},{6,30},{7,31},{8,0},{9,1... | collective-permute-start | bytes 196616 | tf_op jit(solution)/shard_map/ppermute | solution.py:29
  165.2 6.1 %collective-permute-start.31 = (bf16[64,512]{1,0:T(8,128)(2,1)S(1)}, bf16[64,512]{1,0:T(8,128)(2,1)S(1)}, u32[]{:S(2)}, u32[]{:S(2)}) collective-permute-start(bf16[64,512]{1,0:T(8,128)(2,1)S(1)} %get-tuple-element.13), channel_id=1, source_target_pairs={{0,8},{1,9},{2,10},{3,11},{4,12},{5,13},{6,14},{7,15},{8,16},{9,17... | collective-permute-start | bytes 196616 | tf_op jit(solution)/shard_map/ppermute | solution.py:29
  166.7 6.1 %collective-permute-start.32 = (bf16[64,512]{1,0:T(8,128)(2,1)S(1)}, bf16[64,512]{1,0:T(8,128)(2,1)S(1)}, u32[]{:S(2)}, u32[]{:S(2)}) collective-permute-start(bf16[64,512]{1,0:T(8,128)(2,1)S(1)} %get-tuple-element.13), channel_id=1, source_target_pairs={{0,16},{1,17},{2,18},{3,19},{4,20},{5,21},{6,22},{7,23},{8,24},{9,... | collective-permute-start | bytes 196616 | tf_op jit(solution)/shard_map/ppermute | solution.py:29
  169.6 4.3 %collective-permute-start.33 = (bf16[64,512]{1,0:T(8,128)(2,1)S(1)}, bf16[64,512]{1,0:T(8,128)(2,1)S(1)}, u32[]{:S(2)}, u32[]{:S(2)}) collective-permute-start(bf16[64,512]{1,0:T(8,128)(2,1)S(1)} %get-tuple-element.13), channel_id=1, source_target_pairs={{0,24},{1,25},{2,26},{3,27},{4,28},{5,29},{6,30},{7,31},{8,0},{9,1... | collective-permute-start | bytes 196616 | tf_op jit(solution)/shard_map/ppermute | solution.py:29
  174.8 5.4 %collective-permute-start.36 = (f32[64,256]{1,0:T(8,128)S(1)}, f32[64,256]{1,0:T(8,128)S(1)}, u32[]{:S(2)}, u32[]{:S(2)}) collective-permute-start(f32[64,256]{1,0:T(8,128)S(1)} %get-tuple-element.9), channel_id=1, source_target_pairs={{0,1},{1,0},{2,3},{3,2},{4,5},{5,4},{6,7},{7,6},{8,9},{9,8},{10,11... | collective-permute-start | bytes 196616 | tf_op jit(solution)/shard_map/ppermute | solution.py:29
  174.9 4.0 %collective-permute-start.37 = (bf16[64,256]{1,0:T(8,128)(2,1)S(1)}, bf16[64,256]{1,0:T(8,128)(2,1)S(1)}, u32[]{:S(2)}, u32[]{:S(2)}) collective-permute-start(bf16[64,256]{1,0:T(8,128)(2,1)S(1)} %get-tuple-element.33), channel_id=1, source_target_pairs={{0,4},{1,5},{2,6},{3,7},{4,0},{5,1},{6,2},{7,3},{8,12},{9,13},{10,... | collective-permute-start | bytes 98312 | tf_op jit(solution)/shard_map/ppermute | solution.py:29
  176.8 3.3 %collective-permute-start.38 = (bf16[64,256]{1,0:T(8,128)(2,1)S(1)}, bf16[64,256]{1,0:T(8,128)(2,1)S(1)}, u32[]{:S(2)}, u32[]{:S(2)}) collective-permute-start(bf16[64,256]{1,0:T(8,128)(2,1)S(1)} %get-tuple-element.32), channel_id=1, source_target_pairs={{0,5},{1,4},{2,7},{3,6},{4,1},{5,0},{6,3},{7,2},{8,13},{9,12},{10,... | collective-permute-start | bytes 98312 | tf_op jit(solution)/shard_map/ppermute | solution.py:29
